TPU v7x, 64 devices: a 2x2x8 block of a 4x4x8 slice. The times are simulated.
64 devices in a mesh: dp: 4 (over x, y), ep: 16 (over z, core).
Axes of the slice: x: 2, y: 2, z: 8, core: 2. Of those that a mesh axis runs over, the one named last changes fastest.
The devices are a block of a 4x4x8 slice.
Arguments:
- x_in: bfloat16 [49152, 512], P(('dp', 'ep')), parts along dimension 0
- grad_y: bfloat16 [49152, 512], P(('dp', 'ep')), parts along dimension 0
- ids_a: int32 [49152, 6], P(('dp', 'ep')), parts along dimension 0
- gate_a: float32 [49152, 6], P(('dp', 'ep')), parts along dimension 0
- ids_b: int32 [49152, 6], P(('dp', 'ep')), parts along dimension 0
- gate_b: float32 [49152, 6], P(('dp', 'ep')), parts along dimension 0
- w1_a: bfloat16 [64, 512, 384], P('ep')
- w3_a: bfloat16 [64, 512, 384], P('ep')
- w2_a: bfloat16 [64, 384, 512], P('ep')
- w1_b: bfloat16 [64, 512, 384], P('ep')
- w3_b: bfloat16 [64, 512, 384], P('ep')
- w2_b: bfloat16 [64, 384, 512], P('ep')
- wg_mid: bfloat16 [512, 2752], replicated
- wu_mid: bfloat16 [512, 2752], replicated
- wd_mid: bfloat16 [2752, 512], replicated
- wg_top: bfloat16 [512, 2752], replicated
- wu_top: bfloat16 [512, 2752], replicated
- wd_top: bfloat16 [2752, 512], replicated
Outputs:
- output 1: bfloat16 [49152, 512], P(('dp', 'ep')), parts along dimension 0
- output 2: bfloat16 [49152, 512], P(('dp', 'ep')), parts along dimension 0
- output 3: float32 [256, 512, 384], P(('dp', 'ep')), parts along dimension 0
- output 4: float32 [256, 512, 384], P(('dp', 'ep')), parts along dimension 0
- output 5: float32 [256, 384, 512], P(('dp', 'ep')), parts along dimension 0
- output 6: float32 [256, 512, 384], P(('dp', 'ep')), parts along dimension 0
- output 7: float32 [256, 512, 384], P(('dp', 'ep')), parts along dimension 0
- output 8: float32 [256, 384, 512], P(('dp', 'ep')), parts along dimension 0
- output 9: float32 [49152, 6], P(('dp', 'ep')), parts along dimension 0
- output 10: float32 [49152, 6], P(('dp', 'ep')), parts along dimension 0
There are 4 independent parts. A program takes and returns all parts, laid end to end along the dimension named above; an argument that names none is the same for every part.
All inputs are finite; a program needn't handle non-finite values.
Results may differ from a plain program's by a relative error of at most 0.02.
Values are sent between devices in bfloat16 or wider.
A program may use at most 768 MiB of HBM per device.

v0:
```python
import jax
import jax.numpy as jnp
from jax import lax
from jax.sharding import PartitionSpec as P

CONTRACT_LAST = (((1,), (1,)), ((), ()))


def route_pairs(expert_ids, n_exp, capacity):
    n_tok, top_k = expert_ids.shape
    flat_ids = expert_ids.reshape(-1)
    onehot = (flat_ids[:, None] == jnp.arange(n_exp, dtype=jnp.int32)[None, :]).astype(jnp.int32)
    slots = jnp.sum((jnp.cumsum(onehot, axis=0) - onehot) * onehot, axis=1)
    pair_rows = flat_ids * capacity + slots
    filler = jnp.full((n_exp * capacity,), n_tok * top_k, jnp.int32)
    filler = filler.at[pair_rows].set(jnp.arange(n_tok * top_k, dtype=jnp.int32))
    return pair_rows, filler


def swiglu_grad(pre_gate, pre_up, grad_hidden):
    sigma = jax.nn.sigmoid(pre_gate)
    grad_gate = grad_hidden * pre_up * sigma * (1.0 + pre_gate * (1.0 - sigma))
    grad_up = grad_hidden * pre_gate * sigma
    return grad_gate.astype(jnp.bfloat16), grad_up.astype(jnp.bfloat16)


def dense_forward(x_rows, w_gate, w_up, w_down):
    pre_gate = jnp.dot(x_rows, w_gate, preferred_element_type=jnp.float32)
    pre_up = jnp.dot(x_rows, w_up, preferred_element_type=jnp.float32)
    hidden = (jax.nn.silu(pre_gate) * pre_up).astype(jnp.bfloat16)
    branch = jnp.dot(hidden, w_down, preferred_element_type=jnp.float32)
    return (x_rows.astype(jnp.float32) + branch).astype(jnp.bfloat16)


def dense_backward(x_rows, grad_out, w_gate, w_up, w_down):
    pre_gate = jnp.dot(x_rows, w_gate, preferred_element_type=jnp.float32)
    pre_up = jnp.dot(x_rows, w_up, preferred_element_type=jnp.float32)
    grad_hidden = lax.dot_general(grad_out, w_down, CONTRACT_LAST, preferred_element_type=jnp.float32)
    grad_gate, grad_up = swiglu_grad(pre_gate, pre_up, grad_hidden)
    branch = (lax.dot_general(grad_gate, w_gate, CONTRACT_LAST, preferred_element_type=jnp.float32)
              + lax.dot_general(grad_up, w_up, CONTRACT_LAST, preferred_element_type=jnp.float32))
    return (grad_out.astype(jnp.float32) + branch).astype(jnp.bfloat16)


def expert_forward(tokens, w_one, w_three, w_two):
    pre_gate = jnp.einsum('secd,edf->secf', tokens, w_one, preferred_element_type=jnp.float32)
    pre_up = jnp.einsum('secd,edf->secf', tokens, w_three, preferred_element_type=jnp.float32)
    hidden = (jax.nn.silu(pre_gate) * pre_up).astype(jnp.bfloat16)
    return jnp.einsum('secf,efd->secd', hidden, w_two, preferred_element_type=jnp.float32).astype(jnp.bfloat16)


def expert_backward(tokens, grad_rows, gate_rows, w_one, w_three, w_two):
    pre_gate = jnp.einsum('secd,edf->secf', tokens, w_one, preferred_element_type=jnp.float32)
    pre_up = jnp.einsum('secd,edf->secf', tokens, w_three, preferred_element_type=jnp.float32)
    hidden = (jax.nn.silu(pre_gate) * pre_up).astype(jnp.bfloat16)
    out_rows = jnp.einsum('secf,efd->secd', hidden, w_two, preferred_element_type=jnp.float32).astype(jnp.bfloat16)
    grad_mix = jnp.sum(grad_rows.astype(jnp.float32) * out_rows.astype(jnp.float32), axis=-1)
    grad_out = (gate_rows[..., None] * grad_rows).astype(jnp.bfloat16)
    grad_w_two = jnp.einsum('secf,secd->efd', hidden, grad_out, preferred_element_type=jnp.float32)
    grad_hidden = jnp.einsum('secd,efd->secf', grad_out, w_two, preferred_element_type=jnp.float32)
    grad_gate, grad_up = swiglu_grad(pre_gate, pre_up, grad_hidden)
    grad_w_one = jnp.einsum('secd,secf->edf', tokens, grad_gate, preferred_element_type=jnp.float32)
    grad_w_three = jnp.einsum('secd,secf->edf', tokens, grad_up, preferred_element_type=jnp.float32)
    grad_tokens = (jnp.einsum('secf,edf->secd', grad_gate, w_one, preferred_element_type=jnp.float32)
                   + jnp.einsum('secf,edf->secd', grad_up, w_three, preferred_element_type=jnp.float32)).astype(jnp.bfloat16)
    return grad_tokens, grad_mix, grad_w_one, grad_w_three, grad_w_two


def solution(mesh):
    group = mesh.shape['ep']
    tok_spec = P(('dp', 'ep'), None)
    exp_spec = P('ep', None, None)
    full_spec = P(None, None)
    grad_spec = P(('dp', 'ep'), None, None)

    def device_program(x_in, grad_y, ids_a, gate_a, ids_b, gate_b, w1_a, w3_a, w2_a, w1_b, w3_b, w2_b,
                       wg_mid, wu_mid, wd_mid, wg_top, wu_top, wd_top):
        n_tok, hidden_dim = x_in.shape
        top_k = ids_a.shape[1]
        n_local = w1_a.shape[0]
        n_exp = n_local * group
        capacity = 2 * n_tok * top_k // n_exp

        def send_rows(rows, filler):
            picked = jnp.take(rows, filler // top_k, axis=0, mode='fill', fill_value=0)
            return lax.all_to_all(picked.reshape(group, n_local, capacity, hidden_dim), 'ep', 0, 0, tiled=True)

        def send_gates(gate, filler):
            picked = jnp.take(gate.reshape(-1), filler, axis=0, mode='fill', fill_value=0)
            return lax.all_to_all(picked.reshape(group, n_local, capacity), 'ep', 0, 0, tiled=True)

        def return_rows(expert_rows, pair_rows):
            returned = lax.all_to_all(expert_rows, 'ep', 0, 0, tiled=True)
            flat_rows = returned.reshape((n_exp * capacity,) + returned.shape[3:])
            return jnp.take(flat_rows, pair_rows, axis=0).reshape((n_tok, top_k) + returned.shape[3:])

        def combine(x_rows, gate, out_pairs):
            return (x_rows.astype(jnp.float32) + jnp.sum(gate[:, :, None] * out_pairs, axis=1)).astype(jnp.bfloat16)

        def moe_backward(tokens, grad_out, gate, pair_rows, filler, w_one, w_three, w_two):
            grad_rows = send_rows(grad_out, filler)
            gate_rows = send_gates(gate, filler)
            grad_tokens, grad_mix, grad_one, grad_three, grad_two = expert_backward(
                tokens, grad_rows, gate_rows, w_one, w_three, w_two)
            grad_pairs = return_rows(grad_tokens, pair_rows)
            grad_gate = return_rows(grad_mix, pair_rows)
            grad_in = (grad_out.astype(jnp.float32) + jnp.sum(grad_pairs, axis=1, dtype=jnp.float32)).astype(jnp.bfloat16)
            return grad_in, grad_one, grad_three, grad_two, grad_gate

        rows_a, filler_a = route_pairs(ids_a, n_exp, capacity)
        rows_b, filler_b = route_pairs(ids_b, n_exp, capacity)

        tokens_a = send_rows(x_in, filler_a)
        x_a = combine(x_in, gate_a, return_rows(expert_forward(tokens_a, w1_a, w3_a, w2_a), rows_a))
        x_mid = dense_forward(x_a, wg_mid, wu_mid, wd_mid)
        tokens_b = send_rows(x_mid, filler_b)
        x_b = combine(x_mid, gate_b, return_rows(expert_forward(tokens_b, w1_b, w3_b, w2_b), rows_b))
        y_out = dense_forward(x_b, wg_top, wu_top, wd_top)

        grad_b = dense_backward(x_b, grad_y, wg_top, wu_top, wd_top)
        redone_b = send_rows(x_mid, filler_b)
        grad_mid, dw1_b, dw3_b, dw2_b, dgate_b = moe_backward(redone_b, grad_b, gate_b, rows_b, filler_b, w1_b, w3_b, w2_b)
        grad_a = dense_backward(x_a, grad_mid, wg_mid, wu_mid, wd_mid)
        dx_in, dw1_a, dw3_a, dw2_a, dgate_a = moe_backward(tokens_a, grad_a, gate_a, rows_a, filler_a, w1_a, w3_a, w2_a)
        return y_out, dx_in, dw1_a, dw3_a, dw2_a, dw1_b, dw3_b, dw2_b, dgate_a, dgate_b

    in_specs = (tok_spec, tok_spec, tok_spec, tok_spec, tok_spec, tok_spec,
                exp_spec, exp_spec, exp_spec, exp_spec, exp_spec, exp_spec,
                full_spec, full_spec, full_spec, full_spec, full_spec, full_spec)
    out_specs = (tok_spec, tok_spec, grad_spec, grad_spec, grad_spec, grad_spec, grad_spec, grad_spec, tok_spec, tok_spec)
    return jax.shard_map(device_program, mesh=mesh, in_specs=in_specs, out_specs=out_specs, check_vma=False)
```

profile of v0, /device:TPU:22, one launch (start us, length us, event | category | flops | bytes accessed | tf_op | source)
XLA Modules:
  0.0 2496.2 jit_solution(1456702775485897444)
XLA Ops:
  4.6 35.6 %reduce-window.14 = s32[64,36,128]{2,1,0:T(8,128)} reduce-window(s32[64,36,128]{2,1,0:T(8,128)} %fusion.88, s32[]{:T(128)} %constant.80.clone.1), window={size=1x1x128 pad=0_0x0_0x127_0}, to_apply=%region_0.0 | reduce-window | flops 37453824 | bytes 2359300 | tf_op jit(solution)/shard_map/reduce-window
  47.1 17.4 scatter_custom_fusion
  65.2 39.1 %gather_fusion = bf16[9216,512]{1,0:T(8,128)(2,1)} fusion(bf16[768,512]{1,0:T(8,128)(2,1)} %param.26, s32[9216]{0:T(1024)S(1)} %get-tuple-element.65), kind=kCustom, calls=%fused_computation.clone | custom fusion | bytes 18911232 | tf_op jit(solution)/shard_map/jit(_take)/gather | solution.py:85
  111.7 217.8 %all_to_all.61 = bf16[16,4,144,512]{3,2,1,0:T(8,128)(2,1)S(1)} all-to-all(bf16[16,4,144,512]{3,2,1,0:T(8,128)(2,1)S(1)} %bitcast.237), channel_id=1, replica_groups=mesh['dp'=4,'ep'=16] {'ep'}, dimensions={0} | all-to-all | bytes 18874368 | tf_op jit(solution)/shard_map/all_to_all | solution.py:86
  333.1 8.2 fusion.32
  341.3 14.8 fusion.19
  356.1 9.9 convert_bitcast_fusion.1
  365.9 8.2 copy.130
  383.8 35.6 %reduce-window.16 = s32[64,36,128]{2,1,0:T(8,128)} reduce-window(s32[64,36,128]{2,1,0:T(8,128)} %fusion.89, s32[]{:T(128)} %constant.80.clone.1), window={size=1x1x128 pad=0_0x0_0x127_0}, to_apply=%region_5.8 | reduce-window | flops 37453824 | bytes 2359300 | tf_op jit(solution)/shard_map/reduce-window.2
  426.2 17.6 scatter_custom_fusion.1
  444.0 148.1 %all-to-all-done.1 = bf16[16,4,144,512]{3,2,1,0:T(8,128)(2,1)} async-done(((bf16[16,4,144,512]{3,2,1,0:T(8,128)(2,1)}), bf16[16,4,144,512]{3,2,1,0:T(8,128)(2,1)}, u32[]{:S(2)}, u32[]{:S(2)}) %all-to-all-start.1) | async-done | bytes 9437216 | tf_op jit(solution)/shard_map/all_to_all | solution.py:93
  592.1 18.9 gather_fusion.1
  618.3 11.4 reshape.215
  629.7 7.7 multiply_reduce_fusion.1
  647.7 39.3 %gather_fusion.2 = bf16[9216,512]{1,0:T(8,128)(2,1)} fusion(bf16[768,512]{1,0:T(8,128)(2,1)} %add_convert_fusion.8, s32[9216]{0:T(1024)S(1)} %get-tuple-element.63), kind=kCustom, calls=%fused_computation.4.clone | custom fusion | bytes 18911232 | tf_op jit(solution)/shard_map/jit(_take)/gather | solution.py:85
  694.4 215.3 %all_to_all.62 = bf16[16,4,144,512]{3,2,1,0:T(8,128)(2,1)S(1)} all-to-all(bf16[16,4,144,512]{3,2,1,0:T(8,128)(2,1)S(1)} %bitcast.238), channel_id=1, replica_groups=mesh['dp'=4,'ep'=16] {'ep'}, dimensions={0} | all-to-all | bytes 18874368 | tf_op jit(solution)/shard_map/all_to_all | solution.py:86
  913.4 8.2 fusion.28
  921.6 14.8 fusion.14
  936.4 9.9 convert_bitcast_fusion
  946.3 8.2 copy.139
  960.3 51.2 %gather_fusion.4 = f32[9216]{0:T(1024)S(1)} fusion(f32[4608]{0:T(1024)S(1)} %reshape.203, s32[9216]{0:T(1024)S(1)} %get-tuple-element.62), kind=kCustom, calls=%fused_computation.2.clone | custom fusion | bytes 110592 | tf_op jit(solution)/shard_map/jit(_take)/gather | solution.py:89
  1012.3 7.7 fusion.117
  1019.9 152.5 %all-to-all-done.3 = bf16[16,4,144,512]{3,2,1,0:T(8,128)(2,1)} async-done(((bf16[16,4,144,512]{3,2,1,0:T(8,128)(2,1)}), bf16[16,4,144,512]{3,2,1,0:T(8,128)(2,1)}, u32[]{:S(2)}, u32[]{:S(2)}) %all-to-all-start.3) | async-done | bytes 9437216 | tf_op jit(solution)/shard_map/all_to_all | solution.py:93
  1172.5 8.1 all-to-all-start.4
  1180.6 18.9 gather_fusion.3
  1206.7 11.3 reshape.216
  1218.1 7.6 multiply_reduce_fusion
  1239.7 10.6 add_convert_fusion.5
  1250.3 37.7 %gather_fusion.5 = bf16[9216,512]{1,0:T(8,128)(2,1)} fusion(bf16[768,512]{1,0:T(8,128)(2,1)S(1)} %add_convert_fusion.5, s32[9216]{0:T(1024)S(1)} %get-tuple-element.63), kind=kCustom, calls=%fused_computation.5.clone | custom fusion | bytes 18911232 | tf_op jit(solution)/shard_map/jit(_take)/gather | solution.py:85
  1288.0 11.3 broadcast_select_fusion
  1306.8 212.5 %all-to-all-done.5 = bf16[16,4,144,512]{3,2,1,0:T(8,128)(2,1)} async-done(((bf16[16,4,144,512]{3,2,1,0:T(8,128)(2,1)}), bf16[16,4,144,512]{3,2,1,0:T(8,128)(2,1)}, u32[]{:S(2)}, u32[]{:S(2)}) %all-to-all-start.5) | async-done | bytes 9437216 | tf_op jit(solution)/shard_map/all_to_all | solution.py:86
  1519.3 21.8 fusion.13
  1541.1 12.3 fusion.83
  1553.5 13.5 fusion.24
  1566.9 8.2 copy.143
  1575.1 8.0 all-to-all-start.6
  1583.4 51.2 %gather_fusion.7 = f32[9216]{0:T(1024)S(1)} fusion(f32[4608]{0:T(1024)S(1)} %reshape.207, s32[9216]{0:T(1024)S(1)} %copy-done.40), kind=kCustom, calls=%fused_computation.10.clone | custom fusion | bytes 110592 | tf_op jit(solution)/shard_map/jit(_take)/gather | solution.py:89
  1635.4 160.3 %all-to-all-done.6 = bf16[16,4,144,512]{3,2,1,0:T(8,128)(2,1)} async-done(((bf16[16,4,144,512]{3,2,1,0:T(8,128)(2,1)}), bf16[16,4,144,512]{3,2,1,0:T(8,128)(2,1)}, u32[]{:S(2)}, u32[]{:S(2)}) %all-to-all-start.6) | async-done | bytes 9437216 | tf_op jit(solution)/shard_map/all_to_all | solution.py:93
  1795.6 8.1 all-to-all-start.7
  1803.8 18.9 gather_fusion.6
  1830.0 11.3 reshape.217
  1841.3 8.5 reduce_sum.82
  1863.8 11.0 add_convert_fusion.3
  1874.9 37.7 %gather_fusion.8 = bf16[9216,512]{1,0:T(8,128)(2,1)} fusion(bf16[768,512]{1,0:T(8,128)(2,1)S(1)} %add_convert_fusion.3, s32[9216]{0:T(1024)S(1)} %copy-done.34), kind=kCustom, calls=%fused_computation.6.clone | custom fusion | bytes 18911232 | tf_op jit(solution)/shard_map/jit(_take)/gather | solution.py:85
  1912.6 11.4 broadcast_select_fusion.2
  1931.5 9.1 fusion.1
  1941.3 202.7 %all-to-all-done.8 = bf16[16,4,144,512]{3,2,1,0:T(8,128)(2,1)} async-done(((bf16[16,4,144,512]{3,2,1,0:T(8,128)(2,1)}), bf16[16,4,144,512]{3,2,1,0:T(8,128)(2,1)}, u32[]{:S(2)}, u32[]{:S(2)}) %all-to-all-start.8) | async-done | bytes 9437216 | tf_op jit(solution)/shard_map/all_to_all | solution.py:86
  2144.0 8.1 all-to-all-start.11
  2152.1 9.1 fusion.3
  2161.2 21.9 fusion.8
  2183.0 12.2 fusion.76
  2203.5 13.9 fusion.25
  2217.4 8.2 copy.147
  2233.2 10.1 add_convert_fusion.6
  2243.4 9.4 fusion.68
  2252.8 9.0 fusion.62
  2268.8 24.1 gather_fusion.11
  2294.0 9.4 fusion.71
  2303.4 11.2 fusion.56
  2321.6 24.1 gather_fusion.10
  2346.8 98.9 %all-to-all-done.9 = bf16[16,4,144,512]{3,2,1,0:T(8,128)(2,1)} async-done(((bf16[16,4,144,512]{3,2,1,0:T(8,128)(2,1)}), bf16[16,4,144,512]{3,2,1,0:T(8,128)(2,1)}, u32[]{:S(2)}, u32[]{:S(2)}) %all-to-all-start.9) | async-done | bytes 9437216 | tf_op jit(solution)/shard_map/all_to_all | solution.py:93
  2445.7 18.9 gather_fusion.9
  2471.9 11.7 reshape.218
  2483.6 9.7 reduce_sum.83
  (226 shorter events, 175.1 us)
Async XLA Ops:
  0.6 1225.4 %copy-start = (bf16[512,2752]{0,1:T(8,128)(2,1)S(1)}, bf16[512,2752]{0,1:T(8,128)(2,1)}, u32[]{:S(2)}) copy-start(bf16[512,2752]{0,1:T(8,128)(2,1)} %param.42) | copy-start | bytes 8454148
  64.5 39.8 %copy-start.31 = (s32[9216]{0:T(1024)}, s32[9216]{0:T(1024)S(1)}, u32[]{:S(2)}) copy-start(s32[9216]{0:T(1024)S(1)} %scatter_custom_fusion) | copy-start | bytes 110596
  65.1 39.2 %copy-start.33 = (s32[9216]{0:T(1024)}, s32[9216]{0:T(1024)S(1)}, u32[]{:S(2)}) copy-start(s32[9216]{0:T(1024)S(1)} %get-tuple-element.65) | copy-start | bytes 110596
  65.2 39.1 %copy-start.42 = (pred[9216]{0:T(1024)(128)(4,1)}, pred[9216]{0:T(1024)(128)(4,1)S(1)}, u32[]{:S(2)}) copy-start(pred[9216]{0:T(1024)(128)(4,1)S(1)} %compare_and_fusion.1) | copy-start | bytes 27652
  111.7 221.4 %copy-start.16 = (bf16[4,512,384]{2,1,0:T(8,128)(2,1)S(1)}, bf16[4,512,384]{2,1,0:T(8,128)(2,1)}, u32[]{:S(2)}) copy-start(bf16[4,512,384]{2,1,0:T(8,128)(2,1)} %param.32) | copy-start | bytes 4718596
  333.1 8.2 copy-start.29
  374.1 6.1 copy-start.53
  374.1 218.0 %all-to-all-start.1 = ((bf16[16,4,144,512]{3,2,1,0:T(8,128)(2,1)}), bf16[16,4,144,512]{3,2,1,0:T(8,128)(2,1)}, u32[]{:S(2)}, u32[]{:S(2)}) async-start(bf16[16,4,144,512]{3,2,1,0:T(8,128)(2,1)} %copy.130), calls=%async_computation.1 | async-start | bytes 18874368 | tf_op jit(solution)/shard_map/all_to_all | solution.py:93
  380.4 249.3 %copy-start.19 = (f32[768,6]{1,0:T(8,128)}, f32[768,6]{1,0:T(8,128)S(1)}, u32[]{:S(2)}) copy-start(f32[768,6]{1,0:T(8,128)S(1)} %copy.122) | copy-start | bytes 55300
  443.8 167.2 %copy-start.46 = (pred[4608]{0:T(1024)(128)(4,1)}, pred[4608]{0:T(1024)(128)(4,1)S(1)}, u32[]{:S(2)}) copy-start(pred[4608]{0:T(1024)(128)(4,1)S(1)} %get-tuple-element.56) | copy-start | bytes 13828
  443.9 167.2 %copy-start.35 = (s32[5120]{0:T(1024)}, s32[5120]{0:T(1024)S(1)}, u32[]{:S(2)}) copy-start(s32[5120]{0:T(1024)S(1)} %pad_clamp_fusion.1) | copy-start | bytes 61444
  443.9 243.1 %copy-start.44 = (pred[9216]{0:T(1024)(128)(4,1)}, pred[9216]{0:T(1024)(128)(4,1)S(1)}, u32[]{:S(2)}) copy-start(pred[9216]{0:T(1024)(128)(4,1)S(1)} %compare_and_fusion) | copy-start | bytes 27652
  629.7 7.8 copy-start.2
  629.7 8.1 copy-start.23
  640.2 7.6 copy-start.9
  694.4 219.0 %copy-start.14 = (bf16[4,512,384]{2,1,0:T(8,128)(2,1)S(1)}, bf16[4,512,384]{2,1,0:T(8,128)(2,1)}, u32[]{:S(2)}) copy-start(bf16[4,512,384]{2,1,0:T(8,128)(2,1)} %param.35) | copy-start | bytes 4718596
  913.4 8.2 copy-start.27
  954.5 218.0 %all-to-all-start.3 = ((bf16[16,4,144,512]{3,2,1,0:T(8,128)(2,1)}), bf16[16,4,144,512]{3,2,1,0:T(8,128)(2,1)}, u32[]{:S(2)}, u32[]{:S(2)}) async-start(bf16[16,4,144,512]{3,2,1,0:T(8,128)(2,1)} %copy.139), calls=%async_computation.3 | async-start | bytes 18874368 | tf_op jit(solution)/shard_map/all_to_all | solution.py:93
  1012.2 187.2 %copy-start.48 = (pred[4608]{0:T(1024)(128)(4,1)}, pred[4608]{0:T(1024)(128)(4,1)S(1)}, u32[]{:S(2)}) copy-start(pred[4608]{0:T(1024)(128)(4,1)S(1)} %get-tuple-element.54) | copy-start | bytes 13828
  1012.3 187.2 %copy-start.37 = (s32[5120]{0:T(1024)}, s32[5120]{0:T(1024)S(1)}, u32[]{:S(2)}) copy-start(s32[5120]{0:T(1024)S(1)} %pad_clamp_fusion) | copy-start | bytes 61444
  1172.5 126.8 %all-to-all-start.4 = ((f32[16,4,144]{2,1,0:T(4,128)}), f32[16,4,144]{2,1,0:T(4,128)S(1)}, u32[]{:S(2)}, u32[]{:S(2)}) async-start(f32[16,4,144]{2,1,0:T(4,128)} %reshape.204), calls=%async_computation.4 | async-start | bytes 131072 | tf_op jit(solution)/shard_map/all_to_all | solution.py:90
  1218.1 7.7 copy-start.4
  1228.4 11.2 copy-start.7
  1250.3 37.7 %copy-start.45 = (pred[9216]{0:T(1024)(128)(4,1)S(1)}, pred[9216]{0:T(1024)(128)(4,1)}, u32[]{:S(2)}) copy-start(pred[9216]{0:T(1024)(128)(4,1)} %copy-done.44) | copy-start | bytes 27652
  1299.3 220.0 %all-to-all-start.5 = ((bf16[16,4,144,512]{3,2,1,0:T(8,128)(2,1)}), bf16[16,4,144,512]{3,2,1,0:T(8,128)(2,1)}, u32[]{:S(2)}, u32[]{:S(2)}) async-start(bf16[16,4,144,512]{3,2,1,0:T(8,128)(2,1)} %bitcast.236), calls=%async_computation.5 | async-start | bytes 18874368 | tf_op jit(solution)/shard_map/all_to_all | solution.py:86
  1306.8 234.3 %copy-start.51 = (f32[16,4,144]{2,0,1:T(8,128)}, f32[16,4,144]{2,0,1:T(8,128)S(1)}, u32[]{:S(2)}) copy-start(f32[16,4,144]{2,0,1:T(8,128)S(1)} %copy.141) | copy-start | bytes 110596
  1519.3 21.8 copy-start.15
  1541.1 12.4 copy-start.28
  1575.1 8.0 copy-start.20
  1575.1 8.3 copy-start.40
  1575.1 220.5 %all-to-all-start.6 = ((bf16[16,4,144,512]{3,2,1,0:T(8,128)(2,1)}), bf16[16,4,144,512]{3,2,1,0:T(8,128)(2,1)}, u32[]{:S(2)}, u32[]{:S(2)}) async-start(bf16[16,4,144,512]{3,2,1,0:T(8,128)(2,1)} %copy.143), calls=%async_computation.6 | async-start | bytes 18874368 | tf_op jit(solution)/shard_map/all_to_all | solution.py:93
  1583.4 51.2 %copy-start.32 = (s32[9216]{0:T(1024)S(1)}, s32[9216]{0:T(1024)}, u32[]{:S(2)}) copy-start(s32[9216]{0:T(1024)} %copy-done.31) | copy-start | bytes 110596
  1583.4 220.4 %copy-start.38 = (s32[5120]{0:T(1024)S(1)}, s32[5120]{0:T(1024)}, u32[]{:S(2)}) copy-start(s32[5120]{0:T(1024)} %copy-done.37) | copy-start | bytes 61444
  1795.6 128.4 %all-to-all-start.7 = ((f32[16,4,144]{2,1,0:T(4,128)}), f32[16,4,144]{2,1,0:T(4,128)S(1)}, u32[]{:S(2)}, u32[]{:S(2)}) async-start(f32[16,4,144]{2,1,0:T(4,128)} %reshape.208), calls=%async_computation.7 | async-start | bytes 131072 | tf_op jit(solution)/shard_map/all_to_all | solution.py:90
  1803.8 18.9 copy-start.49
  1849.8 8.2 copy-start.24
  1849.8 13.9 slice-start.6
  1858.0 5.8 slice-start.8
  1858.0 5.8 copy-start.26
  1863.8 11.1 copy-start.34
  1874.8 37.8 %copy-start.3 = (bf16[768,512]{1,0:T(8,128)(2,1)}, bf16[768,512]{1,0:T(8,128)(2,1)S(1)}, u32[]{:S(2)}) copy-start(bf16[768,512]{1,0:T(8,128)(2,1)S(1)} %add_convert_fusion.3) | copy-start | bytes 2359300
  1874.8 37.8 %copy-start.43 = (pred[9216]{0:T(1024)(128)(4,1)S(1)}, pred[9216]{0:T(1024)(128)(4,1)}, u32[]{:S(2)}) copy-start(pred[9216]{0:T(1024)(128)(4,1)} %copy-done.42) | copy-start | bytes 27652
  1924.0 220.0 %all-to-all-start.8 = ((bf16[16,4,144,512]{3,2,1,0:T(8,128)(2,1)}), bf16[16,4,144,512]{3,2,1,0:T(8,128)(2,1)}, u32[]{:S(2)}, u32[]{:S(2)}) async-start(bf16[16,4,144,512]{3,2,1,0:T(8,128)(2,1)} %bitcast.235), calls=%async_computation.8 | async-start | bytes 18874368 | tf_op jit(solution)/shard_map/all_to_all | solution.py:86
  2144.0 51.9 %all-to-all-start.11 = ((f32[16,4,144]{2,1,0:T(4,128)}), f32[16,4,144]{2,1,0:T(4,128)S(1)}, u32[]{:S(2)}, u32[]{:S(2)}) async-start(f32[16,4,144]{2,1,0:T(4,128)} %copy.153), calls=%async_computation.11 | async-start | bytes 131072 | tf_op jit(solution)/shard_map/all_to_all | solution.py:93
  2161.2 21.9 copy-start.17
  2196.0 29.6 %all-to-all-start.10 = ((f32[16,4,144]{2,1,0:T(4,128)}), f32[16,4,144]{2,1,0:T(4,128)S(1)}, u32[]{:S(2)}, u32[]{:S(2)}) async-start(f32[16,4,144]{2,1,0:T(4,128)} %copy.152), calls=%async_computation.10 | async-start | bytes 131072 | tf_op jit(solution)/shard_map/all_to_all | solution.py:93
  2225.6 7.6 copy-start.13
  2225.6 220.2 %all-to-all-start.9 = ((bf16[16,4,144,512]{3,2,1,0:T(8,128)(2,1)}), bf16[16,4,144,512]{3,2,1,0:T(8,128)(2,1)}, u32[]{:S(2)}, u32[]{:S(2)}) async-start(bf16[16,4,144,512]{3,2,1,0:T(8,128)(2,1)} %copy.147), calls=%async_computation.9 | async-start | bytes 18874368 | tf_op jit(solution)/shard_map/all_to_all | solution.py:93
  2233.2 10.1 copy-start.52
  2233.2 19.6 slice-start.3
  2233.2 19.6 slice-start.4
  2243.4 9.4 slice-start.5
  2243.4 18.5 slice-start.9
  2252.8 9.0 slice-start.10
  2261.9 6.9 copy-start.39
  2268.7 24.1 copy-start.50
  2294.0 20.6 slice-start
  2294.0 20.6 slice-start.1
  2294.0 20.6 slice-start.11
  2303.4 11.2 slice-start.2
  2303.4 11.2 slice-start.12
  2314.7 6.9 copy-start.36
  2321.6 24.1 copy-start.47
  2471.9 24.1 copy-start.1
  (14 other events, 58.5 us)
where the time goes:
time: 2510 us; the launch traced here: 2500 us
  waiting for transfers between devices  975 us (39%)
  local copies, waits for them, and re-layouts  529 us (21%)
  blocking collectives  433 us (17%)
  matrix products  282 us (11%)
  other arithmetic  201 us (8%)
  starting transfers between devices  73.2 us (3%)
    all_to_all x6, waiting for transfers between devices, return_rows(): returned = lax.all_to_all(expert_rows, 'ep', 0, 0, tiled=True)  560 us
    all_to_all x2, blocking collectives, send_rows(): lax.all_to_all(picked.reshape(group, n_local, capacity, hidden_dim), 'ep'...  433 us
    all_to_all x2, waiting for transfers between devices, send_rows(): lax.all_to_all(picked.reshape(group, n_local, capacity, hidden_dim), 'ep'...  415 us
    gather x4, local copies, waits for them, and re-layouts, send_rows(): picked = jnp.take(rows, filler // top_k, axis=0, mode='fill', fill_value=0)  154 us
    gather x6, local copies, waits for them, and re-layouts, return_rows(): jnp.take(flat_rows, pair_rows, axis=0)  124 us
    gather x2, local copies, waits for them, and re-layouts, send_gates(): jnp.take(gate.reshape(-1), filler, axis=0, mode='fill', fill_value=0)  102 us
    another operation x6, other arithmetic  74.8 us
  transfers between devices with their start and end apart: 10, of which 6 were waited for; matrix products, arithmetic and copies ran while one was open for 24% of the time, Pallas kernels for 0%

commit v1 on v0

v1 whole, which is shorter than its diff:
```python
import functools

import jax
import jax.numpy as jnp
from jax import lax
from jax.experimental import pallas as pl
from jax.experimental.pallas import tpu as pltpu
from jax.sharding import PartitionSpec as P

CONTRACT_LAST = (((1,), (1,)), ((), ()))
CONTRACT_FIRST = (((0,), (0,)), ((), ()))
F32 = jnp.float32
BF16 = jnp.bfloat16


def dot(a, b, dims=(((1,), (0,)), ((), ()))):
    return lax.dot_general(a, b, dims, preferred_element_type=F32)


def swiglu_grad(pre_gate, pre_up, grad_hidden):
    sigma = jax.nn.sigmoid(pre_gate)
    grad_gate = grad_hidden * pre_up * sigma * (1.0 + pre_gate * (1.0 - sigma))
    grad_up = grad_hidden * pre_gate * sigma
    return grad_gate.astype(BF16), grad_up.astype(BF16)


def dense_forward(x_rows, w_gate, w_up, w_down):
    pre_gate = dot(x_rows, w_gate)
    pre_up = dot(x_rows, w_up)
    hidden = (jax.nn.silu(pre_gate) * pre_up).astype(BF16)
    branch = dot(hidden, w_down)
    return (x_rows.astype(F32) + branch).astype(BF16)


def dense_backward(x_rows, grad_out, w_gate, w_up, w_down):
    pre_gate = dot(x_rows, w_gate)
    pre_up = dot(x_rows, w_up)
    grad_hidden = dot(grad_out, w_down, CONTRACT_LAST)
    grad_gate, grad_up = swiglu_grad(pre_gate, pre_up, grad_hidden)
    branch = dot(grad_gate, w_gate, CONTRACT_LAST) + dot(grad_up, w_up, CONTRACT_LAST)
    return (grad_out.astype(F32) + branch).astype(BF16)


def pick_rows(meta, expert, capacity):
    n_tok = meta.shape[1]
    slots = lax.broadcasted_iota(jnp.int32, (capacity, n_tok), 0).astype(F32)
    return meta[expert:expert + 1, :] == slots


def place_rows(meta_t, expert, capacity):
    n_tok = meta_t.shape[0]
    slots = lax.broadcasted_iota(jnp.int32, (n_tok, capacity), 1).astype(F32)
    return jnp.where(meta_t[:, expert:expert + 1] == slots, 1.0, 0.0).astype(BF16)


def pack(meta, n_local, capacity):
    masks = [jnp.where(pick_rows(meta, e, capacity), 1.0, 0.0).astype(BF16) for e in range(n_local)]
    return jnp.concatenate(masks, axis=0)


def forward_kernel(n_local, capacity, meta_ref, meta_t_ref, x_ref, w1_ref, w3_ref, w2_ref, out_ref, tok, res):
    pair = x_ref.shape[0]
    for i in range(pair):
        tok[i] = dot(pack(meta_ref[i], n_local, capacity), x_ref[i]).astype(BF16)
    for e in range(n_local):
        rows = slice(e * capacity, (e + 1) * capacity)
        a = jnp.concatenate([tok[i, rows] for i in range(pair)], axis=0)
        hidden = (jax.nn.silu(dot(a, w1_ref[e])) * dot(a, w3_ref[e])).astype(BF16)
        o = dot(hidden, w2_ref[e]).astype(BF16)
        for i in range(pair):
            res[i, rows] = o[i * capacity:(i + 1) * capacity]
    for i in range(pair):
        for e in range(n_local):
            part = dot(place_rows(meta_t_ref[i], e, capacity), res[i, e * capacity:(e + 1) * capacity])
            part = meta_t_ref[i, :, n_local + e:n_local + e + 1] * part
            out_ref[i] = part if e == 0 else out_ref[i] + part


def backward_kernel(n_local, capacity, meta_ref, meta_t_ref, x_ref, c_ref, w1_ref, w3_ref, w2_ref,
                    out_ref, mix_ref, dw1_ref, dw3_ref, dw2_ref, tok, cot, res):
    pair = x_ref.shape[0]

    @pl.when(pl.program_id(0) == 0)
    def _():
        dw1_ref[...] = jnp.zeros_like(dw1_ref)
        dw3_ref[...] = jnp.zeros_like(dw3_ref)
        dw2_ref[...] = jnp.zeros_like(dw2_ref)

    for i in range(pair):
        picked = pack(meta_ref[i], n_local, capacity)
        tok[i] = dot(picked, x_ref[i]).astype(BF16)
        cot[i] = dot(picked, c_ref[i]).astype(BF16)
    for e in range(n_local):
        rows = slice(e * capacity, (e + 1) * capacity)
        a = jnp.concatenate([tok[i, rows] for i in range(pair)], axis=0)
        c = jnp.concatenate([cot[i, rows] for i in range(pair)], axis=0)
        gate = jnp.concatenate(
            [jnp.sum(jnp.where(pick_rows(meta_ref[i], e, capacity), meta_ref[i, n_local + e:n_local + e + 1, :], 0.0),
                     axis=1, keepdims=True) for i in range(pair)], axis=0)
        pre_gate = dot(a, w1_ref[e])
        pre_up = dot(a, w3_ref[e])
        hidden = (jax.nn.silu(pre_gate) * pre_up).astype(BF16)
        o = dot(hidden, w2_ref[e]).astype(BF16)
        cf = c.astype(F32)
        mix = jnp.sum(cf * o.astype(F32), axis=1, keepdims=True)
        for i in range(pair):
            own = mix[i * capacity:(i + 1) * capacity]
            mix_ref[i, e:e + 1, :] = jnp.sum(jnp.where(pick_rows(meta_ref[i], e, capacity), own, 0.0), axis=0, keepdims=True)
        grad_o = (gate * cf).astype(BF16)
        dw2_ref[e] += dot(hidden, grad_o, CONTRACT_FIRST)
        grad_hidden = dot(grad_o, w2_ref[e], CONTRACT_LAST)
        grad_gate, grad_up = swiglu_grad(pre_gate, pre_up, grad_hidden)
        dw1_ref[e] += dot(a, grad_gate, CONTRACT_FIRST)
        dw3_ref[e] += dot(a, grad_up, CONTRACT_FIRST)
        du = (dot(grad_gate, w1_ref[e], CONTRACT_LAST) + dot(grad_up, w3_ref[e], CONTRACT_LAST)).astype(BF16)
        for i in range(pair):
            res[i, rows] = du[i * capacity:(i + 1) * capacity]
    for i in range(pair):
        placed = jnp.concatenate([place_rows(meta_t_ref[i], e, capacity) for e in range(n_local)], axis=1)
        out_ref[i] = dot(placed, res[i])


def whole(shape):
    return pl.BlockSpec(shape, lambda g: (0,) * len(shape))


def chunk(shape):
    return pl.BlockSpec(shape, lambda g: (g,) + (0,) * (len(shape) - 1))


PAIR = 2


def expert_forward(meta, meta_t, x_all, w1, w3, w2, capacity):
    group, n_tok, width = x_all.shape
    n_local, _, ff = w1.shape
    packed = n_local * capacity
    return pl.pallas_call(
        functools.partial(forward_kernel, n_local, capacity),
        grid=(group // PAIR,),
        in_specs=[chunk((PAIR,) + meta.shape[1:]), chunk((PAIR,) + meta_t.shape[1:]), chunk((PAIR, n_tok, width)),
                  whole(w1.shape), whole(w3.shape), whole(w2.shape)],
        out_specs=chunk((PAIR, n_tok, width)),
        out_shape=jax.ShapeDtypeStruct((group, n_tok, width), F32),
        scratch_shapes=[pltpu.VMEM((PAIR, packed, width), BF16)] * 2,
        compiler_params=pltpu.CompilerParams(vmem_limit_bytes=60 * 1024 * 1024),
        cost_estimate=pl.CostEstimate(flops=40 * 10**9, bytes_accessed=40 * 10**6, transcendentals=0),
        name="expert_forward",
    )(meta, meta_t, x_all, w1, w3, w2)


def expert_backward(meta, meta_t, x_all, c_all, w1, w3, w2, capacity):
    group, n_tok, width = x_all.shape
    n_local, _, ff = w1.shape
    packed = n_local * capacity
    return pl.pallas_call(
        functools.partial(backward_kernel, n_local, capacity),
        grid=(group // PAIR,),
        in_specs=[chunk((PAIR,) + meta.shape[1:]), chunk((PAIR,) + meta_t.shape[1:]),
                  chunk((PAIR, n_tok, width)), chunk((PAIR, n_tok, width)),
                  whole(w1.shape), whole(w3.shape), whole(w2.shape)],
        out_specs=[chunk((PAIR, n_tok, width)), chunk((PAIR, n_local, n_tok)),
                   whole(w1.shape), whole(w3.shape), whole(w2.shape)],
        out_shape=[jax.ShapeDtypeStruct((group, n_tok, width), F32), jax.ShapeDtypeStruct((group, n_local, n_tok), F32),
                   jax.ShapeDtypeStruct(w1.shape, F32), jax.ShapeDtypeStruct(w3.shape, F32),
                   jax.ShapeDtypeStruct(w2.shape, F32)],
        scratch_shapes=[pltpu.VMEM((PAIR, packed, width), BF16)] * 3,
        compiler_params=pltpu.CompilerParams(vmem_limit_bytes=60 * 1024 * 1024),
        cost_estimate=pl.CostEstimate(flops=80 * 10**9, bytes_accessed=60 * 10**6, transcendentals=0),
        name="expert_backward",
    )(meta, meta_t, x_all, c_all, w1, w3, w2)


def solution(mesh):
    group = mesh.shape['ep']
    tok_spec = P(('dp', 'ep'), None)
    exp_spec = P('ep', None, None)
    full_spec = P(None, None)
    grad_spec = P(('dp', 'ep'), None, None)

    def device_program(x_in, grad_y, ids_a, gate_a, ids_b, gate_b, w1_a, w3_a, w2_a, w1_b, w3_b, w2_b,
                       wg_mid, wu_mid, wd_mid, wg_top, wu_top, wd_top):
        n_tok, width = x_in.shape
        top_k = ids_a.shape[1]
        n_local = w1_a.shape[0]
        n_exp = n_local * group
        capacity = 2 * n_tok * top_k // n_exp
        me = lax.axis_index('ep')

        heads = jnp.concatenate([ids_a.astype(F32), gate_a, ids_b.astype(F32), gate_b], axis=1).T
        heads = lax.all_gather(heads, 'ep', axis=0, tiled=False)
        mine = (me * n_local + jnp.arange(n_local, dtype=jnp.int32)).astype(F32)
        earlier = jnp.triu(jnp.ones((n_tok, n_tok), BF16), 1)

        def route(ids, gate):
            match = ids[:, None, :, :] == mine[None, :, None, None]
            chosen = jnp.any(match, axis=2)
            gates = jnp.sum(jnp.where(match, gate[:, None, :, :], 0.0), axis=2)
            before = dot(chosen.astype(BF16).reshape(group * n_local, n_tok), earlier).reshape(chosen.shape)
            meta = jnp.concatenate([jnp.where(chosen, before, -1.0), gates], axis=1)
            return meta, jnp.swapaxes(meta, 1, 2)

        meta_a, meta_at = route(heads[:, :top_k], heads[:, top_k:2 * top_k])
        meta_b, meta_bt = route(heads[:, 2 * top_k:3 * top_k], heads[:, 3 * top_k:])

        def gather(rows):
            return lax.all_gather(rows, 'ep', axis=0, tiled=False)

        def scatter_sum(parts):
            return lax.psum_scatter(parts.reshape(group * n_tok, width), 'ep', scatter_dimension=0, tiled=True)

        def add_rows(rows, total):
            return (rows.astype(F32) + total).astype(BF16)

        def return_mix(mix, ids):
            home = lax.all_to_all(mix, 'ep', 0, 0, tiled=True).reshape(n_exp, n_tok)
            picked = ids.T[:, None, :] == jnp.arange(n_exp, dtype=jnp.int32)[None, :, None]
            return jnp.sum(jnp.where(picked, home[None], 0.0), axis=1).T

        x_a = add_rows(x_in, scatter_sum(expert_forward(meta_a, meta_at, gather(x_in), w1_a, w3_a, w2_a, capacity)))
        x_mid = dense_forward(x_a, wg_mid, wu_mid, wd_mid)
        held_b = gather(x_mid)
        x_b = add_rows(x_mid, scatter_sum(expert_forward(meta_b, meta_bt, held_b, w1_b, w3_b, w2_b, capacity)))
        y_out = dense_forward(x_b, wg_top, wu_top, wd_top)

        x_b, grad_y, y_out = lax.optimization_barrier((x_b, grad_y, y_out))
        grad_b = dense_backward(x_b, grad_y, wg_top, wu_top, wd_top)
        part_b, mix_b, dw1_b, dw3_b, dw2_b = expert_backward(
            meta_b, meta_bt, held_b, gather(grad_b), w1_b, w3_b, w2_b, capacity)
        x_again, grad_b2 = lax.optimization_barrier((x_in, grad_b))
        held_a = gather(x_again)
        grad_mid = add_rows(grad_b2, scatter_sum(part_b))
        grad_a = dense_backward(x_a, grad_mid, wg_mid, wu_mid, wd_mid)
        part_a, mix_a, dw1_a, dw3_a, dw2_a = expert_backward(
            meta_a, meta_at, held_a, gather(grad_a), w1_a, w3_a, w2_a, capacity)
        dx_in = add_rows(grad_a, scatter_sum(part_a))
        return (y_out, dx_in, dw1_a, dw3_a, dw2_a, dw1_b, dw3_b, dw2_b,
                return_mix(mix_a, ids_a), return_mix(mix_b, ids_b))

    in_specs = (tok_spec, tok_spec, tok_spec, tok_spec, tok_spec, tok_spec,
                exp_spec, exp_spec, exp_spec, exp_spec, exp_spec, exp_spec,
                full_spec, full_spec, full_spec, full_spec, full_spec, full_spec)
    out_specs = (tok_spec, tok_spec, grad_spec, grad_spec, grad_spec, grad_spec, grad_spec, grad_spec, tok_spec, tok_spec)
    return jax.shard_map(device_program, mesh=mesh, in_specs=in_specs, out_specs=out_specs, check_vma=False)
```

time: 2510 us -> 1350 us (0.54)
  local copies, waits for them, and re-layouts: 529 us -> 58.6 us
  blocking collectives: 433 us -> 14.4 us
  Pallas kernels: 0 us -> 285 us
  matrix products: 282 us -> 81.9 us
  waiting for transfers between devices: 975 us -> 820 us
  other arithmetic: 201 us -> 47.3 us
  starting transfers between devices: 73.2 us -> 17.2 us
    all_to_all x10 -> x1, waiting for transfers between devices: 975 us -> 10.2 us  [return_mix(): home = lax.all_to_all(mix, 'ep', 0, 0, tiled=True).reshape(n_exp, n_tok)]
    reduce_scatter x0 -> x4, waiting for transfers between devices: none -> 517 us  [scatter_sum(): lax.psum_scatter(parts.reshape(group * n_tok, width), 'ep', scatter_dimen...]
    all_to_all x2 -> x1, blocking collectives: 433 us -> 14.4 us  [return_mix(): home = lax.all_to_all(mix, 'ep', 0, 0, tiled=True).reshape(n_exp, n_tok)]
    gather x12 -> x0, local copies, waits for them, and re-layouts: 380 us -> none  [the longest x4 154 us: send_rows(): picked = jnp.take(rows, filler // top_k, axis=0, mode='fill', fill_value=0)]
    all_gather x0 -> x6, waiting for transfers between devices: none -> 291 us  [the longest x5 252 us: gather(): return lax.all_gather(rows, 'ep', axis=0, tiled=False)]
    pallas_call x0 -> x4, Pallas kernels: none -> 285 us  [the longest x2 196 us: expert_backward(): pl.pallas_call(functools.partial(backward_kernel, n_local, capacity), gri...]
    dot_general x30 -> x14, matrix products: 282 us -> 81.9 us  [dot(): return lax.dot_general(a, b, dims, preferred_element_type=F32)]
    convert_element_type x8 -> x0, local copies, waits for them, and re-layouts: 78.4 us -> none  [the longest x2 23 us: moe_backward(): jnp.sum(grad_pairs, axis=1, dtype=jnp.float32)]
  transfers between devices with their start and end apart: 10 -> 11, of which waited for: 6 -> 11; matrix products, arithmetic and copies ran while one was open for 24% -> 7% of each run, Pallas kernels for 0% -> 0%
where the time goes in v1:
time: 1350 us; the launch traced here: 1340 us
  waiting for transfers between devices  820 us (61%)
  Pallas kernels  285 us (21%)
  matrix products  81.9 us (6%)
  local copies, waits for them, and re-layouts  58.6 us (4%)
  other arithmetic  47.3 us (4%)
  starting transfers between devices  17.2 us (1%)
  between operations  14.7 us (1%)
  blocking collectives  14.4 us (1%)
    reduce_scatter x4, waiting for transfers between devices, scatter_sum(): lax.psum_scatter(parts.reshape(group * n_tok, width), 'ep', scatter_dimen...  517 us
    all_gather x5, waiting for transfers between devices, gather(): return lax.all_gather(rows, 'ep', axis=0, tiled=False)  252 us
    pallas_call x2, Pallas kernels, expert_backward(): pl.pallas_call(functools.partial(backward_kernel, n_local, capacity), gri...  196 us
    pallas_call x2, Pallas kernels, expert_forward(): pl.pallas_call(functools.partial(forward_kernel, n_local, capacity), grid...  89.2 us
    dot_general x14, matrix products, dot(): return lax.dot_general(a, b, dims, preferred_element_type=F32)  81.9 us
    all_gather x1, waiting for transfers between devices, device_program(): heads = lax.all_gather(heads, 'ep', axis=0, tiled=False)  38.3 us
  transfers between devices with their start and end apart: 11, of which 11 were waited for; matrix products, arithmetic and copies ran while one was open for 7% of the time, Pallas kernels for 0%

profile of v1, /device:TPU:22, one launch (start us, length us, event | category | flops | bytes accessed | tf_op | source)
XLA Modules:
  0.0 1339.2 jit_solution(4760099773148079589)
XLA Ops:
  7.3 0.9 convert_element_type.82
  8.9 1.4 maximum_bitcast_fusion
  11.3 38.3 %all-gather.13.cloned.1.call-done = f32[384,768]{1,0:T(8,128)} async-done(((f32[24,768]{1,0:T(8,128)}), f32[384,768]{1,0:T(8,128)}) %all-gather.13.cloned.1.call-update) | async-done | bytes 1179664 | tf_op jit(solution)/shard_map/all_gather | solution.py:191
  49.6 2.7 fusion.29
  52.8 2.9 copy.41
  55.7 0.9 fusion.12
  56.7 4.7 copy.42
  61.4 1.1 copy.43
  62.5 1.1 copy.49
  63.6 1.0 fusion.7
  64.6 4.8 copy.44
  69.4 4.1 broadcast_select_fusion.1
  73.6 2.6 copy-done.2
  76.2 4.3 pad_maximum_fusion
  80.5 5.1 copy.45.meta_ref
  85.6 9.0 fusion.58.meta_t_ref
  94.6 27.4 %all-gather.15.cloned.1.call-done = bf16[12288,512]{1,0:T(8,128)(2,1)} async-done(((bf16[768,512]{1,0:T(8,128)(2,1)}), bf16[12288,512]{1,0:T(8,128)(2,1)}) %all-gather.15.cloned.1.call-update) | async-done | bytes 12582928 | tf_op jit(solution)/shard_map/all_gather | solution.py:207
  122.0 44.6 %expert_forward.2 = f32[16,768,512]{2,1,0:T(8,128)} custom-call(f32[16,8,768]{2,1,0:T(8,128)} %copy.45.meta_ref, f32[16,768,8]{2,1,0:T(8,128)} %fusion.58.meta_t_ref, bf16[16,768,512]{2,1,0:T(8,128)(2,1)} %bitcast.60, bf16[4,512,384]{2,1,0:T(8,128)(2,1)} %w1_ref.7, bf16[4,512,384]{2,1,0:T(8,128)(2,1)} %w3_ref.7, bf16[4,384,512]{2,1,0:T(8,128)(2,1)} %w2_ref.7), custom_call_target="tpu_custom_call" | custom-call | flops 40000000000 | bytes 40000000 | tf_op jit(solution)/shard_map/expert_forward/pallas_call | solution.py:138
  166.7 11.3 all-gather.17.cloned.1.call-start
  178.0 127.1 %reduce-scatter.5.cloned.1.call-done = f32[768,512]{1,0:T(8,128)} async-done(((f32[12288,512]{1,0:T(8,128)}), f32[768,512]{1,0:T(8,128)}) %reduce-scatter.5.cloned.1.call-update) | async-done | bytes 1572880 | tf_op jit(solution)/shard_map/reduce_scatter | solution.py:210
  305.1 1.9 add_convert_fusion.7
  307.0 4.4 fusion.30
  311.4 2.4 fusion.31
  313.8 1.4 copy-done.6
  315.2 3.3 copy-done.7
  318.5 3.6 add_convert_fusion.6
  322.2 2.9 copy.47
  325.4 4.0 copy.48
  329.4 3.9 copy.50
  333.3 4.1 broadcast_select_fusion
  337.4 2.6 copy-done.3
  340.1 4.3 pad_maximum_fusion.1
  344.4 5.1 copy.51.meta_ref
  349.5 9.0 fusion.59.meta_t_ref
  358.5 34.7 %all-gather.17.cloned.1.call-done = bf16[12288,512]{1,0:T(8,128)(2,1)} async-done(((bf16[768,512]{1,0:T(8,128)(2,1)}), bf16[12288,512]{1,0:T(8,128)(2,1)}) %all-gather.17.cloned.1.call-update) | async-done | bytes 12582928 | tf_op jit(solution)/shard_map/all_gather | solution.py:207
  393.2 44.6 %expert_forward.3 = f32[16,768,512]{2,1,0:T(8,128)} custom-call(f32[16,8,768]{2,1,0:T(8,128)} %copy.51.meta_ref, f32[16,768,8]{2,1,0:T(8,128)} %fusion.59.meta_t_ref, bf16[16,768,512]{2,1,0:T(8,128)(2,1)} %bitcast.58, bf16[4,512,384]{2,1,0:T(8,128)(2,1)} %w1_ref.6, bf16[4,512,384]{2,1,0:T(8,128)(2,1)} %w3_ref.6, bf16[4,384,512]{2,1,0:T(8,128)(2,1)} %w2_ref.6), custom_call_target="tpu_custom_call" | custom-call | flops 40000000000 | bytes 40000000 | tf_op jit(solution)/shard_map/expert_forward/pallas_call | solution.py:138
  438.3 138.0 %reduce-scatter.7.cloned.1.call-done = f32[768,512]{1,0:T(8,128)} async-done(((f32[12288,512]{1,0:T(8,128)}), f32[768,512]{1,0:T(8,128)}) %reduce-scatter.7.cloned.1.call-update) | async-done | bytes 1572880 | tf_op jit(solution)/shard_map/reduce_scatter | solution.py:210
  576.3 1.9 add_convert_fusion.5
  578.2 0.9 copy-done.11
  579.0 5.7 fusion.32
  584.7 14.9 %add_convert_fusion.4 = bf16[768,512]{1,0:T(8,128)(2,1)} fusion(bf16[768,512]{1,0:T(8,128)(2,1)} %copy-done.11, bf16[2752,512]{1,0:T(8,128)(2,1)} %param.35, f32[768,2752]{0,1:T(8,128)} %fusion.32, bf16[512,2752]{0,1:T(8,128)(2,1)} %param.34), kind=kOutput, calls=%fused_computation.24 | convolution fusion | flops 4342382592 | bytes 15663104 | tf_op jit(solution)/shard_map/dot_general | solution.py:17
  599.5 4.5 fusion.33
  604.1 2.6 fusion.34
  606.8 1.2 copy-done.8
  607.9 3.3 copy-done.9
  611.2 3.7 fusion.1
  614.9 17.4 %add_convert_fusion.3 = bf16[768,512]{1,0:T(8,128)(2,1)} fusion(f32[768,512]{1,0:T(8,128)} %fusion.1, bf16[768,512]{1,0:T(8,128)(2,1)} %param.19, bf16[512,2752]{0,1:T(8,128)(2,1)S(1)} %copy-done, f32[768,2752]{0,1:T(8,128)} %copy-done.9, f32[768,2752]{0,1:T(8,128)} %copy-done.8, bf16[768,512]{1,0:T(8,128)(2,1)} %copy-done.11, bf16[512,2752]{0,1:T(8,128)(2,1)} %param.34), kind=kOutput, calls=%fused_computation.23 | convolution fusion | flops 4351229952 | bytes 26476544 | tf_op jit(solution)/shard_map/dot_general | solution.py:17
  632.6 70.7 %all-gather.19.cloned.1.call-done = bf16[12288,512]{1,0:T(8,128)(2,1)} async-done(((bf16[768,512]{1,0:T(8,128)(2,1)}), bf16[12288,512]{1,0:T(8,128)(2,1)}) %all-gather.19.cloned.1.call-update) | async-done | bytes 12582928 | tf_op jit(solution)/shard_map/all_gather | solution.py:207
  703.3 98.0 %expert_backward.2 = (f32[16,768,512]{2,1,0:T(8,128)}, f32[16,4,768]{2,1,0:T(4,128)}, f32[4,512,384]{2,1,0:T(8,128)}, f32[4,512,384]{2,1,0:T(8,128)}, f32[4,384,512]{2,1,0:T(8,128)}) custom-call(f32[16,8,768]{2,1,0:T(8,128)} %copy.51.meta_ref, f32[16,768,8]{2,1,0:T(8,128)} %fusion.59.meta_t_ref, bf16[16,768,512]{2,1,0:T(8,128)(2,1)} %bitcast.59, ...), custom_call_target="tpu_custom_call" | custom-call | flops 80000000000 | bytes 60000000 | tf_op jit(solution)/shard_map/expert_backward/pallas_call | solution.py:156
  802.7 137.0 %reduce-scatter.9.cloned.1.call-done = f32[768,512]{1,0:T(8,128)} async-done(((f32[12288,512]{1,0:T(8,128)}), f32[768,512]{1,0:T(8,128)}) %reduce-scatter.9.cloned.1.call-update) | async-done | bytes 1572880 | tf_op jit(solution)/shard_map/reduce_scatter | solution.py:210
  939.7 4.9 fusion.28
  944.6 3.2 copy-done.10
  947.9 5.3 fusion.2
  953.8 11.4 add_convert_fusion.1
  965.6 46.6 %all-gather.21.cloned.1.call-done = bf16[12288,512]{1,0:T(8,128)(2,1)} async-done(((bf16[768,512]{1,0:T(8,128)(2,1)}), bf16[12288,512]{1,0:T(8,128)(2,1)}) %all-gather.21.cloned.1.call-update) | async-done | bytes 12582928 | tf_op jit(solution)/shard_map/all_gather | solution.py:207
  1012.2 73.0 %all-gather.23.cloned.1.call-done = bf16[12288,512]{1,0:T(8,128)(2,1)} async-done(((bf16[768,512]{1,0:T(8,128)(2,1)}), bf16[12288,512]{1,0:T(8,128)(2,1)}) %all-gather.23.cloned.1.call-update) | async-done | bytes 12582928 | tf_op jit(solution)/shard_map/all_gather | solution.py:207
  1085.2 98.0 %expert_backward.3 = (f32[16,768,512]{2,1,0:T(8,128)}, f32[16,4,768]{2,1,0:T(4,128)}, f32[4,512,384]{2,1,0:T(8,128)}, f32[4,512,384]{2,1,0:T(8,128)}, f32[4,384,512]{2,1,0:T(8,128)}) custom-call(f32[16,8,768]{2,1,0:T(8,128)} %copy.45.meta_ref, f32[16,768,8]{2,1,0:T(8,128)} %fusion.58.meta_t_ref, bf16[16,768,512]{2,1,0:T(8,128)(2,1)} %bitcast.61, ...), custom_call_target="tpu_custom_call" | custom-call | flops 80000000000 | bytes 60000000 | tf_op jit(solution)/shard_map/expert_backward/pallas_call | solution.py:156
  1183.3 0.8 copy-done.20
  1184.2 14.4 %all_to_all.10 = f32[16,4,768]{2,1,0:T(4,128)S(1)} all-to-all(f32[16,4,768]{2,1,0:T(4,128)S(1)} %copy-done.20), channel_id=1, replica_groups=mesh['dp'=4,'ep'=16] {'ep'}, dimensions={0} | all-to-all | bytes 393216 | tf_op jit(solution)/shard_map/all_to_all | solution.py:216
  1198.6 4.2 all-to-all-start
  1203.6 10.2 all-to-all-done
  1213.9 0.8 select_reduce_fusion.1
  1214.7 114.7 %reduce-scatter.11.cloned.1.call-done = f32[768,512]{1,0:T(8,128)} async-done(((f32[12288,512]{1,0:T(8,128)}), f32[768,512]{1,0:T(8,128)}) %reduce-scatter.11.cloned.1.call-update) | async-done | bytes 1572880 | tf_op jit(solution)/shard_map/reduce_scatter | solution.py:210
  1329.4 2.7 add_convert_fusion
  (74 shorter events, 6.8 us)
Async XLA Ops:
  7.2 571.8 %copy-start = (bf16[512,2752]{0,1:T(8,128)(2,1)S(1)}, bf16[512,2752]{0,1:T(8,128)(2,1)}, u32[]{:S(2)}) copy-start(bf16[512,2752]{0,1:T(8,128)(2,1)} %param.33) | copy-start | bytes 8454148
  7.2 42.4 %all-gather.13.cloned.1.call-start = ((), (), s32[]{:S(2)}) async-start(), calls=%async_computation.10 | async-start | bytes 1253376 | tf_op jit(solution)/shard_map/all_gather | solution.py:191
  10.4 111.6 %all-gather.15.cloned.1.call-start = ((), (), s32[]{:S(2)}) async-start(), calls=%async_computation.11 | async-start | bytes 13369344 | tf_op jit(solution)/shard_map/all_gather | solution.py:207
  11.2 293.9 %reduce-scatter.5.cloned.1.call-start = ((), (), s32[]{:S(2)}) async-start(), calls=%async_computation.6 | async-start | bytes 26738688 | tf_op jit(solution)/shard_map/reduce_scatter | solution.py:210
  69.4 6.8 copy-start.4
  73.6 2.6 copy-start.2
  166.7 226.5 %all-gather.17.cloned.1.call-start = ((), (), s32[]{:S(2)}) async-start(), calls=%async_computation.12 | async-start | bytes 13369344 | tf_op jit(solution)/shard_map/all_gather | solution.py:207
  307.0 4.4 copy-start.15
  311.4 3.8 copy-start.6
  311.4 7.1 copy-start.14
  315.2 3.3 copy-start.7
  322.2 254.1 %reduce-scatter.7.cloned.1.call-start = ((), (), s32[]{:S(2)}) async-start(), calls=%async_computation.7 | async-start | bytes 26738688 | tf_op jit(solution)/shard_map/reduce_scatter | solution.py:210
  325.1 4.2 copy-start.19
  333.3 6.8 copy-start.5
  337.4 2.6 copy-start.3
  437.8 265.5 %all-gather.19.cloned.1.call-start = ((), (), s32[]{:S(2)}) async-start(), calls=%async_computation.13 | async-start | bytes 13369344 | tf_op jit(solution)/shard_map/all_gather | solution.py:207
  578.1 0.9 copy-start.11
  599.5 4.6 copy-start.12
  604.1 3.8 copy-start.8
  604.1 7.1 copy-start.23
  607.9 3.3 copy-start.9
  632.3 307.4 %reduce-scatter.9.cloned.1.call-start = ((), (), s32[]{:S(2)}) async-start(), calls=%async_computation.8 | async-start | bytes 26738688 | tf_op jit(solution)/shard_map/reduce_scatter | solution.py:210
  801.3 138.4 %copy-start.13 = (bf16[768,512]{1,0:T(8,128)(2,1)S(1)}, bf16[768,512]{1,0:T(8,128)(2,1)}, u32[]{:S(2)}) copy-start(bf16[768,512]{1,0:T(8,128)(2,1)} %add_convert_fusion.3) | copy-start | bytes 2359300
  801.4 210.8 %all-gather.21.cloned.1.call-start = ((), (), s32[]{:S(2)}) async-start(), calls=%async_computation.14 | async-start | bytes 13369344 | tf_op jit(solution)/shard_map/all_gather | solution.py:207
  802.2 283.0 %all-gather.23.cloned.1.call-start = ((), (), s32[]{:S(2)}) async-start(), calls=%async_computation.15 | async-start | bytes 13369344 | tf_op jit(solution)/shard_map/all_gather | solution.py:207
  939.7 8.1 copy-start.16
  939.7 13.5 %slice-start = ((s8[8454144]{0:T(1024)(128)(4,1)}), s8[4194304]{0:T(1024)(128)(4,1)S(1)}, s32[]{:S(2)}) async-start(s8[8454144]{0:T(1024)(128)(4,1)} %bitcast.51), calls=%async_computation.16 | async-start | bytes 8388608
  944.6 3.3 copy-start.10
  947.8 5.4 slice-start.1
  947.8 5.4 slice-start.2
  947.8 5.6 copy-start.17
  947.8 6.0 copy-start.18
  965.3 364.1 %reduce-scatter.11.cloned.1.call-start = ((), (), s32[]{:S(2)}) async-start(), calls=%async_computation.9 | async-start | bytes 26738688 | tf_op jit(solution)/shard_map/reduce_scatter | solution.py:210
  1183.2 0.9 copy-start.20
  1183.2 19.6 %copy-start.21 = (s32[768,6]{0,1:T(8,128)S(1)}, s32[768,6]{0,1:T(8,128)}, u32[]{:S(2)}) copy-start(s32[768,6]{0,1:T(8,128)} %param.22) | copy-start | bytes 55300
  1183.3 30.7 %copy-start.22 = (s32[768,6]{0,1:T(8,128)S(1)}, s32[768,6]{0,1:T(8,128)}, u32[]{:S(2)}) copy-start(s32[768,6]{0,1:T(8,128)} %param.20) | copy-start | bytes 55300
  1183.3 148.8 %copy-start.1 = (bf16[512,2752]{0,1:T(8,128)(2,1)S(1)}, bf16[512,2752]{0,1:T(8,128)(2,1)}, u32[]{:S(2)}) copy-start(bf16[512,2752]{0,1:T(8,128)(2,1)} %param.33) | copy-start | bytes 8454148
  1198.6 15.2 %all-to-all-start = ((f32[16,4,768]{2,1,0:T(4,128)}), f32[16,4,768]{2,1,0:T(4,128)S(1)}, u32[]{:S(2)}, u32[]{:S(2)}) async-start(f32[16,4,768]{2,1,0:T(4,128)} %get-tuple-element.38), calls=%async_computation.4 | async-start | bytes 393216 | tf_op jit(solution)/shard_map/all_to_all | solution.py:216
Sparse Core Ops, SparseCore 0:
  10.5 39.0 all-gather.12
  51.2 70.7 all-gather.14
  166.8 138.2 reduce-scatter.4
  322.3 70.8 all-gather.16
  438.0 138.2 reduce-scatter.6
  632.5 70.7 all-gather.18
  801.5 138.1 reduce-scatter.8
  941.3 70.8 all-gather.20
  1014.4 70.7 all-gather.22
  1183.5 145.9 reduce-scatter.10

commit v2 on v1

--- a/solution.py
+++ b/solution.py
@@ -76,9 +76,63 @@
             out_ref[i] = part if e == 0 else out_ref[i] + part
 
 
-def backward_kernel(n_local, capacity, meta_ref, meta_t_ref, x_ref, c_ref, w1_ref, w3_ref, w2_ref,
-                    out_ref, mix_ref, dw1_ref, dw3_ref, dw2_ref, tok, cot, res):
-    pair = x_ref.shape[0]
+def recompute_kernel(n_local, capacity, meta_ref, *refs):
+    *x_refs, w1_ref, w3_ref, w2_ref, tok_ref, gate_ref, up_ref, hid_ref, o_ref = refs
+    pair = meta_ref.shape[0]
+    for i in range(pair):
+        x = jnp.concatenate([x_ref[i] for x_ref in x_refs], axis=0)
+        tok_ref[i] = dot(pack(meta_ref[i], n_local, capacity), x).astype(BF16)
+    for e in range(n_local):
+        rows = slice(e * capacity, (e + 1) * capacity)
+        a = jnp.concatenate([tok_ref[i, rows] for i in range(pair)], axis=0)
+        pre_gate = dot(a, w1_ref[e])
+        pre_up = dot(a, w3_ref[e])
+        hidden = (jax.nn.silu(pre_gate) * pre_up).astype(BF16)
+        o = dot(hidden, w2_ref[e]).astype(BF16)
+        for i in range(pair):
+            own = slice(i * capacity, (i + 1) * capacity)
+            gate_ref[i, rows] = pre_gate[own]
+            up_ref[i, rows] = pre_up[own]
+            hid_ref[i, rows] = hidden[own]
+            o_ref[i, rows] = o[own]
+
+
+def cotangent_kernel(n_local, capacity, meta_ref, meta_t_ref, c_ref, gate_ref, up_ref, o_ref, w1_ref, w3_ref, w2_ref,
+                     out_ref, mix_ref, go_ref, gg_ref, gu_ref, cot, res):
+    pair = c_ref.shape[0]
+    for i in range(pair):
+        cot[i] = dot(pack(meta_ref[i], n_local, capacity), c_ref[i]).astype(BF16)
+    for e in range(n_local):
+        rows = slice(e * capacity, (e + 1) * capacity)
+
+        def both(ref):
+            return jnp.concatenate([ref[i, rows] for i in range(pair)], axis=0)
+
+        cf = both(cot).astype(F32)
+        gate = jnp.concatenate(
+            [jnp.sum(jnp.where(pick_rows(meta_ref[i], e, capacity), meta_ref[i, n_local + e:n_local + e + 1, :], 0.0),
+                     axis=1, keepdims=True) for i in range(pair)], axis=0)
+        mix = jnp.sum(cf * both(o_ref).astype(F32), axis=1, keepdims=True)
+        for i in range(pair):
+            own = mix[i * capacity:(i + 1) * capacity]
+            mix_ref[i, e:e + 1, :] = jnp.sum(jnp.where(pick_rows(meta_ref[i], e, capacity), own, 0.0), axis=0, keepdims=True)
+        grad_o = (gate * cf).astype(BF16)
+        grad_hidden = dot(grad_o, w2_ref[e], CONTRACT_LAST)
+        grad_gate, grad_up = swiglu_grad(both(gate_ref), both(up_ref), grad_hidden)
+        du = (dot(grad_gate, w1_ref[e], CONTRACT_LAST) + dot(grad_up, w3_ref[e], CONTRACT_LAST)).astype(BF16)
+        for i in range(pair):
+            own = slice(i * capacity, (i + 1) * capacity)
+            res[i, rows] = du[own]
+            go_ref[i, rows] = grad_o[own]
+            gg_ref[i, rows] = grad_gate[own]
+            gu_ref[i, rows] = grad_up[own]
+    for i in range(pair):
+        placed = jnp.concatenate([place_rows(meta_t_ref[i], e, capacity) for e in range(n_local)], axis=1)
+        out_ref[i] = dot(placed, res[i])
+
+
+def weight_kernel(n_local, capacity, tok_ref, hid_ref, go_ref, gg_ref, gu_ref, dw1_ref, dw3_ref, dw2_ref):
+    pair = tok_ref.shape[0]
 
     @pl.when(pl.program_id(0) == 0)
     def _():
@@ -86,38 +140,16 @@
         dw3_ref[...] = jnp.zeros_like(dw3_ref)
         dw2_ref[...] = jnp.zeros_like(dw2_ref)
 
-    for i in range(pair):
-        picked = pack(meta_ref[i], n_local, capacity)
-        tok[i] = dot(picked, x_ref[i]).astype(BF16)
-        cot[i] = dot(picked, c_ref[i]).astype(BF16)
     for e in range(n_local):
         rows = slice(e * capacity, (e + 1) * capacity)
-        a = jnp.concatenate([tok[i, rows] for i in range(pair)], axis=0)
-        c = jnp.concatenate([cot[i, rows] for i in range(pair)], axis=0)
-        gate = jnp.concatenate(
-            [jnp.sum(jnp.where(pick_rows(meta_ref[i], e, capacity), meta_ref[i, n_local + e:n_local + e + 1, :], 0.0),
-                     axis=1, keepdims=True) for i in range(pair)], axis=0)
-        pre_gate = dot(a, w1_ref[e])
-        pre_up = dot(a, w3_ref[e])
-        hidden = (jax.nn.silu(pre_gate) * pre_up).astype(BF16)
-        o = dot(hidden, w2_ref[e]).astype(BF16)
-        cf = c.astype(F32)
-        mix = jnp.sum(cf * o.astype(F32), axis=1, keepdims=True)
-        for i in range(pair):
-            own = mix[i * capacity:(i + 1) * capacity]
-            mix_ref[i, e:e + 1, :] = jnp.sum(jnp.where(pick_rows(meta_ref[i], e, capacity), own, 0.0), axis=0, keepdims=True)
-        grad_o = (gate * cf).astype(BF16)
-        dw2_ref[e] += dot(hidden, grad_o, CONTRACT_FIRST)
-        grad_hidden = dot(grad_o, w2_ref[e], CONTRACT_LAST)
-        grad_gate, grad_up = swiglu_grad(pre_gate, pre_up, grad_hidden)
-        dw1_ref[e] += dot(a, grad_gate, CONTRACT_FIRST)
-        dw3_ref[e] += dot(a, grad_up, CONTRACT_FIRST)
-        du = (dot(grad_gate, w1_ref[e], CONTRACT_LAST) + dot(grad_up, w3_ref[e], CONTRACT_LAST)).astype(BF16)
-        for i in range(pair):
-            res[i, rows] = du[i * capacity:(i + 1) * capacity]
-    for i in range(pair):
-        placed = jnp.concatenate([place_rows(meta_t_ref[i], e, capacity) for e in range(n_local)], axis=1)
-        out_ref[i] = dot(placed, res[i])
+
+        def both(ref):
+            return jnp.concatenate([ref[i, rows] for i in range(pair)], axis=0)
+
+        a = both(tok_ref)
+        dw2_ref[e] += dot(both(hid_ref), both(go_ref), CONTRACT_FIRST)
+        dw1_ref[e] += dot(a, both(gg_ref), CONTRACT_FIRST)
+        dw3_ref[e] += dot(a, both(gu_ref), CONTRACT_FIRST)
 
 
 def whole(shape):
@@ -149,26 +181,53 @@
     )(meta, meta_t, x_all, w1, w3, w2)
 
 
-def expert_backward(meta, meta_t, x_all, c_all, w1, w3, w2, capacity):
-    group, n_tok, width = x_all.shape
+def call(kernel, name, ins, outs, scratch, flops):
+    group = ins[0].shape[0]
+
+    def spec(array):
+        return chunk((PAIR,) + array.shape[1:]) if array.shape[0] == group else whole(array.shape)
+
+    return pl.pallas_call(
+        kernel,
+        grid=(group // PAIR,),
+        in_specs=[spec(array) for array in ins],
+        out_specs=[spec(array) for array in outs],
+        out_shape=outs,
+        scratch_shapes=scratch,
+        compiler_params=pltpu.CompilerParams(vmem_limit_bytes=60 * 1024 * 1024),
+        cost_estimate=pl.CostEstimate(flops=flops, bytes_accessed=60 * 10**6, transcendentals=0),
+        name=name,
+    )(*ins)
+
+
+def expert_recompute(meta, pieces, w1, w3, w2, capacity):
+    group, _, width = pieces[0].shape
     n_local, _, ff = w1.shape
     packed = n_local * capacity
-    return pl.pallas_call(
-        functools.partial(backward_kernel, n_local, capacity),
-        grid=(group // PAIR,),
-        in_specs=[chunk((PAIR,) + meta.shape[1:]), chunk((PAIR,) + meta_t.shape[1:]),
-                  chunk((PAIR, n_tok, width)), chunk((PAIR, n_tok, width)),
-                  whole(w1.shape), whole(w3.shape), whole(w2.shape)],
-        out_specs=[chunk((PAIR, n_tok, width)), chunk((PAIR, n_local, n_tok)),
-                   whole(w1.shape), whole(w3.shape), whole(w2.shape)],
-        out_shape=[jax.ShapeDtypeStruct((group, n_tok, width), F32), jax.ShapeDtypeStruct((group, n_local, n_tok), F32),
-                   jax.ShapeDtypeStruct(w1.shape, F32), jax.ShapeDtypeStruct(w3.shape, F32),
-                   jax.ShapeDtypeStruct(w2.shape, F32)],
-        scratch_shapes=[pltpu.VMEM((PAIR, packed, width), BF16)] * 3,
-        compiler_params=pltpu.CompilerParams(vmem_limit_bytes=60 * 1024 * 1024),
-        cost_estimate=pl.CostEstimate(flops=80 * 10**9, bytes_accessed=60 * 10**6, transcendentals=0),
-        name="expert_backward",
-    )(meta, meta_t, x_all, c_all, w1, w3, w2)
+    outs = [jax.ShapeDtypeStruct((group, packed, size), dtype)
+            for size, dtype in ((width, BF16), (ff, F32), (ff, F32), (ff, BF16), (width, BF16))]
+    return call(functools.partial(recompute_kernel, n_local, capacity), "expert_recompute",
+                (meta, *pieces, w1, w3, w2), outs, [], 30 * 10**9)
+
+
+def expert_cotangent(meta, meta_t, c_all, pre_gate, pre_up, o, w1, w3, w2, capacity):
+    group, n_tok, width = c_all.shape
+    n_local, _, ff = w1.shape
+    packed = n_local * capacity
+    outs = [jax.ShapeDtypeStruct((group, n_tok, width), F32), jax.ShapeDtypeStruct((group, n_local, n_tok), F32),
+            jax.ShapeDtypeStruct((group, packed, width), BF16), jax.ShapeDtypeStruct((group, packed, ff), BF16),
+            jax.ShapeDtypeStruct((group, packed, ff), BF16)]
+    return call(functools.partial(cotangent_kernel, n_local, capacity), "expert_cotangent",
+                (meta, meta_t, c_all, pre_gate, pre_up, o, w1, w3, w2), outs,
+                [pltpu.VMEM((PAIR, packed, width), BF16)] * 2, 40 * 10**9)
+
+
+def expert_weights(tok, hidden, grad_o, grad_gate, grad_up, n_local, capacity):
+    width, ff = tok.shape[2], hidden.shape[2]
+    outs = [jax.ShapeDtypeStruct((n_local, width, ff), F32), jax.ShapeDtypeStruct((n_local, width, ff), F32),
+            jax.ShapeDtypeStruct((n_local, ff, width), F32)]
+    return call(functools.partial(weight_kernel, n_local, capacity), "expert_weights",
+                (tok, hidden, grad_o, grad_gate, grad_up), outs, [], 20 * 10**9)
 
 
 def solution(mesh):
@@ -187,12 +246,14 @@
         capacity = 2 * n_tok * top_k // n_exp
         me = lax.axis_index('ep')
 
-        heads = jnp.concatenate([ids_a.astype(F32), gate_a, ids_b.astype(F32), gate_b], axis=1).T
-        heads = lax.all_gather(heads, 'ep', axis=0, tiled=False)
+        def share(ids, gate):
+            return lax.all_gather(jnp.concatenate([ids.astype(F32), gate], axis=1).T, 'ep', axis=0, tiled=False)
+
         mine = (me * n_local + jnp.arange(n_local, dtype=jnp.int32)).astype(F32)
         earlier = jnp.triu(jnp.ones((n_tok, n_tok), BF16), 1)
 
-        def route(ids, gate):
+        def route(heads):
+            ids, gate = heads[:, :top_k], heads[:, top_k:]
             match = ids[:, None, :, :] == mine[None, :, None, None]
             chosen = jnp.any(match, axis=2)
             gates = jnp.sum(jnp.where(match, gate[:, None, :, :], 0.0), axis=2)
@@ -200,9 +261,6 @@
             meta = jnp.concatenate([jnp.where(chosen, before, -1.0), gates], axis=1)
             return meta, jnp.swapaxes(meta, 1, 2)
 
-        meta_a, meta_at = route(heads[:, :top_k], heads[:, top_k:2 * top_k])
-        meta_b, meta_bt = route(heads[:, 2 * top_k:3 * top_k], heads[:, 3 * top_k:])
-
         def gather(rows):
             return lax.all_gather(rows, 'ep', axis=0, tiled=False)
 
@@ -217,23 +275,38 @@
             picked = ids.T[:, None, :] == jnp.arange(n_exp, dtype=jnp.int32)[None, :, None]
             return jnp.sum(jnp.where(picked, home[None], 0.0), axis=1).T
 
-        x_a = add_rows(x_in, scatter_sum(expert_forward(meta_a, meta_at, gather(x_in), w1_a, w3_a, w2_a, capacity)))
+        def backward(meta, meta_t, held, grad_all, w1, w3, w2):
+            tok, pre_gate, pre_up, hidden, o = expert_recompute(meta, held, w1, w3, w2, capacity)
+            part, mix, grad_o, grad_gate, grad_up = expert_cotangent(
+                meta, meta_t, grad_all, pre_gate, pre_up, o, w1, w3, w2, capacity)
+            return part, mix, (tok, hidden, grad_o, grad_gate, grad_up, n_local, capacity)
+
+        meta_a, meta_at = route(share(ids_a, gate_a))
+        held = gather(x_in)
+        part = expert_forward(meta_a, meta_at, held, w1_a, w3_a, w2_a, capacity)
+        ids_late, gate_late, part = lax.optimization_barrier((ids_b, gate_b, part))
+        meta_b, meta_bt = route(share(ids_late, gate_late))
+        x_a = add_rows(x_in, scatter_sum(part))
         x_mid = dense_forward(x_a, wg_mid, wu_mid, wd_mid)
         held_b = gather(x_mid)
         x_b = add_rows(x_mid, scatter_sum(expert_forward(meta_b, meta_bt, held_b, w1_b, w3_b, w2_b, capacity)))
         y_out = dense_forward(x_b, wg_top, wu_top, wd_top)
 
-        x_b, grad_y, y_out = lax.optimization_barrier((x_b, grad_y, y_out))
+        cuts = (n_tok // 4, 3 * (n_tok // 4))
+        x_first, x_second, x_third = x_in[:cuts[0]], x_in[cuts[0]:cuts[1]], x_in[cuts[1]:]
+        x_b, grad_y, x_first = lax.optimization_barrier((x_b, grad_y, x_first))
         grad_b = dense_backward(x_b, grad_y, wg_top, wu_top, wd_top)
-        part_b, mix_b, dw1_b, dw3_b, dw2_b = expert_backward(
-            meta_b, meta_bt, held_b, gather(grad_b), w1_b, w3_b, w2_b, capacity)
-        x_again, grad_b2 = lax.optimization_barrier((x_in, grad_b))
-        held_a = gather(x_again)
-        grad_mid = add_rows(grad_b2, scatter_sum(part_b))
+        grad_b, held_b, x_second, first_a = lax.optimization_barrier((grad_b, held_b, x_second, gather(x_first)))
+        grads_b, y_out = lax.optimization_barrier((gather(grad_b), y_out))
+        part_b, mix_b, for_weights_b = backward(meta_b, meta_bt, (held_b,), grads_b, w1_b, w3_b, w2_b)
+        part_b, second_a = lax.optimization_barrier((part_b, gather(x_second)))
+        total_b, dw1_b, dw3_b, dw2_b = lax.optimization_barrier((scatter_sum(part_b),) + tuple(expert_weights(*for_weights_b)))
+        grad_mid, x_third = lax.optimization_barrier((add_rows(grad_b, total_b), x_third))
         grad_a = dense_backward(x_a, grad_mid, wg_mid, wu_mid, wd_mid)
-        part_a, mix_a, dw1_a, dw3_a, dw2_a = expert_backward(
-            meta_a, meta_at, held_a, gather(grad_a), w1_a, w3_a, w2_a, capacity)
+        grad_a, third_a = lax.optimization_barrier((grad_a, gather(x_third)))
+        part_a, mix_a, for_weights_a = backward(meta_a, meta_at, (first_a, second_a, third_a), gather(grad_a), w1_a, w3_a, w2_a)
         dx_in = add_rows(grad_a, scatter_sum(part_a))
+        dw1_a, dw3_a, dw2_a = expert_weights(*for_weights_a)
         return (y_out, dx_in, dw1_a, dw3_a, dw2_a, dw1_b, dw3_b, dw2_b,
                 return_mix(mix_a, ids_a), return_mix(mix_b, ids_b))
 

time: 1350 us -> 1170 us (0.87)
  waiting for transfers between devices: 820 us -> 575 us
  blocking collectives: 14.4 us -> 60.1 us
  Pallas kernels: 285 us -> 309 us
    all_gather x5 -> x7, waiting for transfers between devices: 252 us -> 95.5 us  [gather(): return lax.all_gather(rows, 'ep', axis=0, tiled=False)]
    all_gather x0 -> x2, blocking collectives: none -> 45.6 us  [share(): lax.all_gather(jnp.concatenate([ids.astype(F32), gate], axis=1).T, 'ep',...]
    reduce_scatter x4, waiting for transfers between devices: 517 us -> 477 us  [scatter_sum(): lax.psum_scatter(parts.reshape(group * n_tok, width), 'ep', scatter_dimen...]
    all_gather x1 -> x0, waiting for transfers between devices: 38.3 us -> none  [device_program(): heads = lax.all_gather(heads, 'ep', axis=0, tiled=False)]
    pallas_call x2 -> x6, Pallas kernels: 196 us -> 220 us  [call(): pl.pallas_call(kernel, grid=(group // PAIR,), in_specs=[spec(array) for a...]
  transfers between devices with their start and end apart: 11 -> 12, of which waited for: 11 -> 10; matrix products, arithmetic and copies ran while one was open for 7% -> 13% of each run, Pallas kernels for 0% -> 15%
where the time goes in v2:
time: 1170 us; the launch traced here: 1160 us
  waiting for transfers between devices  575 us (49%)
  Pallas kernels  309 us (26%)
  matrix products  81.7 us (7%)
  blocking collectives  60.1 us (5%)
  local copies, waits for them, and re-layouts  56 us (5%)
  other arithmetic  53.4 us (5%)
  between operations  14.6 us (1%)
    reduce_scatter x4, waiting for transfers between devices, scatter_sum(): lax.psum_scatter(parts.reshape(group * n_tok, width), 'ep', scatter_dimen...  477 us
    pallas_call x6, Pallas kernels, call(): pl.pallas_call(kernel, grid=(group // PAIR,), in_specs=[spec(array) for a...  220 us
    all_gather x7, waiting for transfers between devices, gather(): return lax.all_gather(rows, 'ep', axis=0, tiled=False)  95.5 us
    pallas_call x2, Pallas kernels, expert_forward(): pl.pallas_call(functools.partial(forward_kernel, n_local, capacity), grid...  89.3 us
    dot_general x14, matrix products, dot(): return lax.dot_general(a, b, dims, preferred_element_type=F32)  81.7 us
    all_gather x2, blocking collectives, share(): lax.all_gather(jnp.concatenate([ids.astype(F32), gate], axis=1).T, 'ep',...  45.6 us
  transfers between devices with their start and end apart: 12, of which 10 were waited for; matrix products, arithmetic and copies ran while one was open for 13% of the time, Pallas kernels for 15%

profile of v2, /device:TPU:22, one launch (start us, length us, event | category | flops | bytes accessed | tf_op | source)
XLA Modules:
  0.0 1156.0 jit_solution(6101205133313199695)
XLA Ops:
  9.6 25.7 %all-gather.9 = f32[16,12,768]{2,1,0:T(8,128)S(1)} all-gather(f32[1,12,768]{2,1,0:T(8,128)S(1)} %maximum_bitcast_fusion), channel_id=2, replica_groups=mesh['dp'=4,'ep'=16] {'ep'}, dimensions={0}, use_global_device_ids=true | all-gather | bytes 626688 | tf_op jit(solution)/shard_map/all_gather | solution.py:250
  35.6 0.9 fusion.7
  36.4 4.8 copy.46
  41.4 2.9 copy.43
  44.6 4.0 copy.44
  48.6 4.0 broadcast_select_fusion.1
  52.6 2.6 copy-done.2
  55.3 7.1 pad_maximum_fusion
  62.3 5.1 copy.47.meta_ref
  67.4 8.9 fusion.62.meta_t_ref
  76.3 11.4 all-gather.19.cloned.1.call-done
  87.7 44.6 %expert_forward.2 = f32[16,768,512]{2,1,0:T(8,128)} custom-call(f32[16,8,768]{2,1,0:T(8,128)} %copy.47.meta_ref, f32[16,768,8]{2,1,0:T(8,128)} %fusion.62.meta_t_ref, bf16[16,768,512]{2,1,0:T(8,128)(2,1)} %bitcast.67, bf16[4,512,384]{2,1,0:T(8,128)(2,1)} %w1_ref.7, bf16[4,512,384]{2,1,0:T(8,128)(2,1)} %w3_ref.7, bf16[4,384,512]{2,1,0:T(8,128)(2,1)} %w2_ref.7), custom_call_target="tpu_custom_call" | custom-call | flops 40000000000 | bytes 40000000 | tf_op jit(solution)/shard_map/expert_forward/pallas_call | solution.py:170
  133.0 137.7 %reduce-scatter.5.cloned.1.call-done = f32[768,512]{1,0:T(8,128)} async-done(((f32[12288,512]{1,0:T(8,128)}), f32[768,512]{1,0:T(8,128)}) %reduce-scatter.5.cloned.1.call-update) | async-done | bytes 1572880 | tf_op jit(solution)/shard_map/reduce_scatter | solution.py:268
  270.7 1.9 add_convert_fusion.7
  272.6 4.4 fusion.32
  277.0 2.4 fusion.31
  279.4 1.4 copy-done.4
  280.8 3.2 copy-done.5
  284.0 3.6 add_convert_fusion.6
  287.8 19.9 %all-gather.10 = f32[16,12,768]{2,1,0:T(8,128)S(1)} all-gather(f32[1,12,768]{2,1,0:T(8,128)S(1)} %maximum_bitcast_fusion.1), channel_id=4, replica_groups=mesh['dp'=4,'ep'=16] {'ep'}, dimensions={0}, use_global_device_ids=true | all-gather | bytes 626688 | tf_op jit(solution)/shard_map/all_gather | solution.py:250
  308.1 4.0 copy.52
  312.4 2.9 copy.49
  315.6 3.9 copy.50
  319.5 4.0 broadcast_select_fusion
  323.5 2.6 copy-done.3
  326.1 7.2 pad_maximum_fusion.1
  333.3 5.1 copy.53.meta_ref
  338.4 8.9 fusion.61.meta_t_ref
  347.2 13.0 %all-gather.21.cloned.1.call-done = bf16[12288,512]{1,0:T(8,128)(2,1)} async-done(((bf16[768,512]{1,0:T(8,128)(2,1)}), bf16[12288,512]{1,0:T(8,128)(2,1)}) %all-gather.21.cloned.1.call-update) | async-done | bytes 12582928 | tf_op jit(solution)/shard_map/all_gather | solution.py:265
  360.2 44.6 %expert_forward.3 = f32[16,768,512]{2,1,0:T(8,128)} custom-call(f32[16,8,768]{2,1,0:T(8,128)} %copy.53.meta_ref, f32[16,768,8]{2,1,0:T(8,128)} %fusion.61.meta_t_ref, bf16[16,768,512]{2,1,0:T(8,128)(2,1)} %bitcast.65, bf16[4,512,384]{2,1,0:T(8,128)(2,1)} %w1_ref.6, bf16[4,512,384]{2,1,0:T(8,128)(2,1)} %w3_ref.6, bf16[4,384,512]{2,1,0:T(8,128)(2,1)} %w2_ref.6), custom_call_target="tpu_custom_call" | custom-call | flops 40000000000 | bytes 40000000 | tf_op jit(solution)/shard_map/expert_forward/pallas_call | solution.py:170
  405.0 1.8 fusion.28
  406.8 137.1 %reduce-scatter.7.cloned.1.call-done = f32[768,512]{1,0:T(8,128)} async-done(((f32[12288,512]{1,0:T(8,128)}), f32[768,512]{1,0:T(8,128)}) %reduce-scatter.7.cloned.1.call-update) | async-done | bytes 1572880 | tf_op jit(solution)/shard_map/reduce_scatter | solution.py:268
  543.9 2.7 add_convert_fusion.5
  546.9 1.8 slice.26
  548.7 4.5 fusion.33
  553.3 2.4 fusion.34
  555.7 1.4 copy-done.7
  557.1 3.2 copy-done.8
  560.3 3.7 fusion.1
  564.0 17.4 %add_convert_fusion.4 = bf16[768,512]{1,0:T(8,128)(2,1)} fusion(f32[768,512]{1,0:T(8,128)} %fusion.1, bf16[768,512]{1,0:T(8,128)(2,1)} %param.19, bf16[512,2752]{0,1:T(8,128)(2,1)S(1)} %copy-done, f32[768,2752]{0,1:T(8,128)} %copy-done.8, f32[768,2752]{0,1:T(8,128)} %copy-done.7, bf16[768,512]{1,0:T(8,128)(2,1)} %add_convert_fusion.5, ...), kind=kOutput, calls=%fused_computation.24 | convolution fusion | flops 4351229952 | bytes 26476544 | tf_op jit(solution)/shard_map/dot_general | solution.py:17
  581.4 1.5 all-gather.23.cloned.1.call-done
  584.1 6.8 fusion.35
  590.9 14.9 %add_convert_fusion.3 = bf16[768,512]{1,0:T(8,128)(2,1)} fusion(bf16[768,512]{1,0:T(8,128)(2,1)} %add_convert_fusion.5, bf16[2752,512]{1,0:T(8,128)(2,1)} %param.35, f32[768,2752]{0,1:T(8,128)} %fusion.35, bf16[512,2752]{0,1:T(8,128)(2,1)} %param.34), kind=kOutput, calls=%fused_computation.23 | convolution fusion | flops 4342382592 | bytes 15663104 | tf_op jit(solution)/shard_map/dot_general | solution.py:17
  605.7 31.9 %expert_recompute.2 = (bf16[16,576,512]{2,1,0:T(8,128)(2,1)}, f32[16,576,384]{2,1,0:T(8,128)}, f32[16,576,384]{2,1,0:T(8,128)}, bf16[16,576,384]{2,1,0:T(8,128)(2,1)}, bf16[16,576,512]{2,1,0:T(8,128)(2,1)}) custom-call(f32[16,8,768]{2,1,0:T(8,128)} %copy.53.meta_ref, bf16[16,768,512]{2,1,0:T(8,128)(2,1)} %bitcast.66, bf16[4,512,384]{2,1,0:T(8,128)(2,1)} %w1_ref.6, ...), custom_call_target="tpu_custom_call" | custom-call | flops 30000001024 | bytes 60000000 | tf_op jit(solution)/shard_map/expert_recompute/pallas_call | solution.py:190
  637.6 17.9 %all-gather.25.cloned.1.call-done = bf16[12288,512]{1,0:T(8,128)(2,1)} async-done(((bf16[768,512]{1,0:T(8,128)(2,1)}), bf16[12288,512]{1,0:T(8,128)(2,1)}) %all-gather.25.cloned.1.call-update) | async-done | bytes 12582928 | tf_op jit(solution)/shard_map/all_gather | solution.py:265
  655.5 47.8 %expert_cotangent.2 = (f32[16,768,512]{2,1,0:T(8,128)}, f32[16,4,768]{2,1,0:T(4,128)}, bf16[16,576,512]{2,1,0:T(8,128)(2,1)}, bf16[16,576,384]{2,1,0:T(8,128)(2,1)}, bf16[16,576,384]{2,1,0:T(8,128)(2,1)}) custom-call(f32[16,8,768]{2,1,0:T(8,128)} %copy.53.meta_ref, f32[16,768,8]{2,1,0:T(8,128)} %fusion.61.meta_t_ref, bf16[16,768,512]{2,1,0:T(8,128)(2,1)} %bitcast.68, ...), custom_call_target="tpu_custom_call" | custom-call | flops 40000000000 | bytes 60000000 | tf_op jit(solution)/shard_map/expert_cotangent/pallas_call | solution.py:190
  703.5 30.3 %expert_weights.2 = (f32[4,512,384]{2,1,0:T(8,128)}, f32[4,512,384]{2,1,0:T(8,128)}, f32[4,384,512]{2,1,0:T(8,128)}) custom-call(bf16[16,576,512]{2,1,0:T(8,128)(2,1)} %get-tuple-element.74.tok_ref, bf16[16,576,384]{2,1,0:T(8,128)(2,1)} %get-tuple-element.75.hid_ref, bf16[16,576,512]{2,1,0:T(8,128)(2,1)} %get-tuple-element.76.go_ref, ...), custom_call_target="tpu_custom_call" | custom-call | flops 20000000000 | bytes 60000000 | tf_op jit(solution)/shard_map/expert_weights/pallas_call | solution.py:190
  733.8 108.0 %reduce-scatter.9.cloned.1.call-done = f32[768,512]{1,0:T(8,128)} async-done(((f32[12288,512]{1,0:T(8,128)}), f32[768,512]{1,0:T(8,128)}) %reduce-scatter.9.cloned.1.call-update) | async-done | bytes 1572880 | tf_op jit(solution)/shard_map/reduce_scatter | solution.py:268
  841.9 1.7 add_convert_fusion.2
  843.9 4.4 fusion.36
  848.3 3.3 copy-done.6
  851.6 5.2 fusion.2
  857.1 11.5 add_convert_fusion.1
  868.6 11.2 all-gather.29.cloned.1.call-done
  880.2 31.8 %expert_recompute.3 = (bf16[16,576,512]{2,1,0:T(8,128)(2,1)}, f32[16,576,384]{2,1,0:T(8,128)}, f32[16,576,384]{2,1,0:T(8,128)}, bf16[16,576,384]{2,1,0:T(8,128)(2,1)}, bf16[16,576,512]{2,1,0:T(8,128)(2,1)}) custom-call(f32[16,8,768]{2,1,0:T(8,128)} %copy.47.meta_ref, bf16[16,192,512]{2,1,0:T(8,128)(2,1)} %bitcast.71, bf16[16,384,512]{2,1,0:T(8,128)(2,1)} %bitcast.70, ...), custom_call_target="tpu_custom_call" | custom-call | flops 30000001024 | bytes 60000000 | tf_op jit(solution)/shard_map/expert_recompute/pallas_call | solution.py:190
  912.0 40.4 %all-gather.31.cloned.1.call-done = bf16[12288,512]{1,0:T(8,128)(2,1)} async-done(((bf16[768,512]{1,0:T(8,128)(2,1)}), bf16[12288,512]{1,0:T(8,128)(2,1)}) %all-gather.31.cloned.1.call-update) | async-done | bytes 12582928 | tf_op jit(solution)/shard_map/all_gather | solution.py:265
  952.4 47.8 %expert_cotangent.3 = (f32[16,768,512]{2,1,0:T(8,128)}, f32[16,4,768]{2,1,0:T(4,128)}, bf16[16,576,512]{2,1,0:T(8,128)(2,1)}, bf16[16,576,384]{2,1,0:T(8,128)(2,1)}, bf16[16,576,384]{2,1,0:T(8,128)(2,1)}) custom-call(f32[16,8,768]{2,1,0:T(8,128)} %copy.47.meta_ref, f32[16,768,8]{2,1,0:T(8,128)} %fusion.62.meta_t_ref, bf16[16,768,512]{2,1,0:T(8,128)(2,1)} %bitcast.69, ...), custom_call_target="tpu_custom_call" | custom-call | flops 40000000000 | bytes 60000000 | tf_op jit(solution)/shard_map/expert_cotangent/pallas_call | solution.py:190
  1000.4 0.8 copy-done.15
  1001.2 14.5 %all_to_all.10 = f32[16,4,768]{2,1,0:T(4,128)S(1)} all-to-all(f32[16,4,768]{2,1,0:T(4,128)S(1)} %copy-done.15), channel_id=1, replica_groups=mesh['dp'=4,'ep'=16] {'ep'}, dimensions={0} | all-to-all | bytes 393216 | tf_op jit(solution)/shard_map/all_to_all | solution.py:274
  1015.8 0.8 select_reduce_fusion
  1016.5 4.3 all-to-all-start
  1020.9 30.4 %expert_weights.3 = (f32[4,512,384]{2,1,0:T(8,128)}, f32[4,512,384]{2,1,0:T(8,128)}, f32[4,384,512]{2,1,0:T(8,128)}) custom-call(bf16[16,576,512]{2,1,0:T(8,128)(2,1)} %get-tuple-element.93.tok_ref, bf16[16,576,384]{2,1,0:T(8,128)(2,1)} %get-tuple-element.94.hid_ref, bf16[16,576,512]{2,1,0:T(8,128)(2,1)} %get-tuple-element.95.go_ref, ...), custom_call_target="tpu_custom_call" | custom-call | flops 20000000000 | bytes 60000000 | tf_op jit(solution)/shard_map/expert_weights/pallas_call | solution.py:190
  1052.1 94.3 %reduce-scatter.11.cloned.1.call-done = f32[768,512]{1,0:T(8,128)} async-done(((f32[12288,512]{1,0:T(8,128)}), f32[768,512]{1,0:T(8,128)}) %reduce-scatter.11.cloned.1.call-update) | async-done | bytes 1572880 | tf_op jit(solution)/shard_map/reduce_scatter | solution.py:268
  1146.4 2.7 add_convert_fusion
  (84 shorter events, 8.3 us)
Async XLA Ops:
  7.2 546.1 %copy-start = (bf16[512,2752]{0,1:T(8,128)(2,1)S(1)}, bf16[512,2752]{0,1:T(8,128)(2,1)}, u32[]{:S(2)}) copy-start(bf16[512,2752]{0,1:T(8,128)(2,1)} %param.33) | copy-start | bytes 8454148
  7.2 80.5 %all-gather.19.cloned.1.call-start = ((), (), s32[]{:S(2)}) async-start(), calls=%async_computation.10 | async-start | bytes 13369344 | tf_op jit(solution)/shard_map/all_gather | solution.py:265
  8.0 262.7 %reduce-scatter.5.cloned.1.call-start = ((), (), s32[]{:S(2)}) async-start(), calls=%async_computation.6 | async-start | bytes 26738688 | tf_op jit(solution)/shard_map/reduce_scatter | solution.py:268
  52.6 2.6 copy-start.2
  132.4 227.8 %all-gather.21.cloned.1.call-start = ((), (), s32[]{:S(2)}) async-start(), calls=%async_computation.11 | async-start | bytes 13369344 | tf_op jit(solution)/shard_map/all_gather | solution.py:265
  272.5 4.4 copy-start.13
  277.0 3.8 copy-start.4
  277.0 7.0 copy-start.11
  280.8 3.2 copy-start.5
  284.0 3.8 copy-start.16
  284.0 3.8 copy-start.19
  287.7 256.2 %reduce-scatter.7.cloned.1.call-start = ((), (), s32[]{:S(2)}) async-start(), calls=%async_computation.7 | async-start | bytes 26738688 | tf_op jit(solution)/shard_map/reduce_scatter | solution.py:268
  323.5 2.6 copy-start.3
  404.9 178.0 %all-gather.23.cloned.1.call-start = ((), (), s32[]{:S(2)}) async-start(), calls=%async_computation.12 | async-start | bytes 3342336 | tf_op jit(solution)/shard_map/all_gather | solution.py:265
  546.7 108.8 %all-gather.25.cloned.1.call-start = ((), (), s32[]{:S(2)}) async-start(), calls=%async_computation.13 | async-start | bytes 13369344 | tf_op jit(solution)/shard_map/all_gather | solution.py:265
  548.7 4.6 copy-start.9
  553.3 3.8 copy-start.7
  553.3 7.1 copy-start.20
  557.1 3.2 copy-start.8
  583.0 120.4 %all-gather.27.cloned.1.call-start = ((), (), s32[]{:S(2)}) async-start(), calls=%async_computation.14 | async-start | bytes 6684672 | tf_op jit(solution)/shard_map/all_gather | solution.py:265
  583.8 258.1 %reduce-scatter.9.cloned.1.call-start = ((), (), s32[]{:S(2)}) async-start(), calls=%async_computation.8 | async-start | bytes 26738688 | tf_op jit(solution)/shard_map/reduce_scatter | solution.py:268
  703.4 176.4 %all-gather.29.cloned.1.call-start = ((), (), s32[]{:S(2)}) async-start(), calls=%async_computation.15 | async-start | bytes 3342336 | tf_op jit(solution)/shard_map/all_gather | solution.py:265
  703.5 138.4 %copy-start.10 = (bf16[768,512]{1,0:T(8,128)(2,1)S(1)}, bf16[768,512]{1,0:T(8,128)(2,1)}, u32[]{:S(2)}) copy-start(bf16[768,512]{1,0:T(8,128)(2,1)} %add_convert_fusion.4) | copy-start | bytes 2359300
  843.6 108.8 %all-gather.31.cloned.1.call-start = ((), (), s32[]{:S(2)}) async-start(), calls=%async_computation.16 | async-start | bytes 13369344 | tf_op jit(solution)/shard_map/all_gather | solution.py:265
  843.9 7.7 copy-start.12
  843.9 12.9 %slice-start = ((s8[8454144]{0:T(1024)(128)(4,1)}), s8[4194304]{0:T(1024)(128)(4,1)S(1)}, s32[]{:S(2)}) async-start(s8[8454144]{0:T(1024)(128)(4,1)} %bitcast.59), calls=%async_computation.17 | async-start | bytes 8388608
  848.3 3.3 copy-start.6
  851.6 5.2 slice-start.1
  851.6 5.2 slice-start.2
  851.6 5.6 copy-start.14
  879.9 266.5 %reduce-scatter.11.cloned.1.call-start = ((), (), s32[]{:S(2)}) async-start(), calls=%async_computation.9 | async-start | bytes 26738688 | tf_op jit(solution)/shard_map/reduce_scatter | solution.py:268
  1000.3 0.9 copy-start.15
  1000.3 15.5 %copy-start.17 = (s32[768,6]{0,1:T(8,128)S(1)}, s32[768,6]{0,1:T(8,128)}, u32[]{:S(2)}) copy-start(s32[768,6]{0,1:T(8,128)} %param.22) | copy-start | bytes 55300
  1016.5 34.8 %all-to-all-start = ((f32[16,4,768]{2,1,0:T(4,128)}), f32[16,4,768]{2,1,0:T(4,128)S(1)}, u32[]{:S(2)}, u32[]{:S(2)}) async-start(f32[16,4,768]{2,1,0:T(4,128)} %get-tuple-element.104), calls=%async_computation.4 | async-start | bytes 393216 | tf_op jit(solution)/shard_map/all_to_all | solution.py:274
  1020.9 30.5 %copy-start.18 = (s32[768,6]{0,1:T(8,128)S(1)}, s32[768,6]{0,1:T(8,128)}, u32[]{:S(2)}) copy-start(s32[768,6]{0,1:T(8,128)} %param.20) | copy-start | bytes 55300
  1020.9 128.3 %copy-start.1 = (bf16[512,2752]{0,1:T(8,128)(2,1)S(1)}, bf16[512,2752]{0,1:T(8,128)(2,1)}, u32[]{:S(2)}) copy-start(bf16[512,2752]{0,1:T(8,128)(2,1)} %param.33) | copy-start | bytes 8454148
Sparse Core Ops, SparseCore 0:
  9.7 78.0 all-gather.18
  132.6 138.0 reduce-scatter.4
  287.8 72.3 all-gather.20
  405.0 138.7 reduce-scatter.6
  546.8 36.0 all-gather.22
  585.0 70.4 all-gather.24
  657.7 41.4 all-gather.26
  703.6 138.2 reduce-scatter.8
  843.7 36.0 all-gather.28
  881.9 70.4 all-gather.30
  1000.5 145.9 reduce-scatter.10
